TPU v7x, 32 devices: a whole 2x2x4 slice. The times are simulated.
32 devices in a mesh: data: 32 (over z, y, x, core).
Axes of the slice: x: 2, y: 2, z: 4, core: 2. Of those that a mesh axis runs over, the one named last changes fastest.
Arguments:
- x_init: bfloat16 [128, 256, 1024], P('data')
- cot_out: bfloat16 [128, 256, 1024], P('data')
- w_query: bfloat16 [2, 1024, 1024], replicated
- w_key: bfloat16 [2, 1024, 1024], replicated
- w_value: bfloat16 [2, 1024, 1024], replicated
- w_proj: bfloat16 [2, 1024, 1024], replicated
- w_up: bfloat16 [1024, 4096], replicated
- w_down: bfloat16 [4096, 1024], replicated
Outputs:
- output 1: float32 [2, 1024, 1024], replicated
- output 2: float32 [2, 1024, 1024], replicated
- output 3: float32 [2, 1024, 1024], replicated
- output 4: float32 [2, 1024, 1024], replicated
- output 5: float32 [1024, 4096], replicated
- output 6: float32 [4096, 1024], replicated
- output 7: bfloat16 [128, 256, 1024], P('data')
All inputs are finite; a program needn't handle non-finite values.
Results may differ from a plain program's by a relative error of at most 0.0195979.
Values are sent between devices in bfloat16 or wider.
A program may use at most 1 GiB of HBM per device.

v0:
```python
import jax
import jax.numpy as jnp
from jax import lax
from jax.sharding import PartitionSpec as P

EPS = 1e-6
HEAD_DIM = 64


def rms_norm(x_f32):
    return x_f32 * lax.rsqrt(jnp.mean(x_f32 * x_f32, axis=-1, keepdims=True) + EPS)


def gelu_tanh(pre_f32):
    return jax.nn.gelu(pre_f32, approximate=True)


def product(subscripts, lhs, rhs):
    return jnp.einsum(subscripts, lhs, rhs, preferred_element_type=jnp.float32)


def layer_forward(x_act, w_query, w_key, w_value, w_proj, w_up, w_down, heads):
    batch, seq_len, width = x_act.shape
    head_dim = width // heads
    x_f32 = x_act.astype(jnp.float32)
    normed = rms_norm(x_f32).astype(jnp.bfloat16)
    query = product("bsd,de->bse", normed, w_query).astype(jnp.bfloat16).reshape(batch, seq_len, heads, head_dim)
    key_act = product("bsd,de->bse", normed, w_key).astype(jnp.bfloat16).reshape(batch, seq_len, heads, head_dim)
    value = product("bsd,de->bse", normed, w_value).astype(jnp.bfloat16).reshape(batch, seq_len, heads, head_dim)
    scores = product("bqhd,bkhd->bhqk", query, key_act) * head_dim ** -0.5
    probs = jax.nn.softmax(scores, axis=-1).astype(jnp.bfloat16)
    mixed = product("bhqk,bkhd->bqhd", probs, value).astype(jnp.bfloat16).reshape(batch, seq_len, width)
    attn_out = product("bsd,de->bse", mixed, w_proj).astype(jnp.bfloat16)
    hidden = (x_f32 + attn_out.astype(jnp.float32)).astype(jnp.bfloat16)
    normed2 = rms_norm(hidden.astype(jnp.float32)).astype(jnp.bfloat16)
    pre_act = product("bsd,df->bsf", normed2, w_up).astype(jnp.bfloat16)
    activated = gelu_tanh(pre_act.astype(jnp.float32)).astype(jnp.bfloat16)
    mlp_out = product("bsf,fd->bsd", activated, w_down).astype(jnp.bfloat16)
    x_next = (hidden.astype(jnp.float32) + mlp_out.astype(jnp.float32)).astype(jnp.bfloat16)
    kept = (x_act, normed, query, key_act, value, probs, mixed, hidden, normed2, pre_act, activated)
    return x_next, kept


def layer_backward(d_next, kept, w_query, w_key, w_value, w_proj, w_up, w_down):
    x_act, normed, query, key_act, value, probs, mixed, hidden, normed2, pre_act, activated = kept
    batch, seq_len, heads, head_dim = query.shape
    width = heads * head_dim
    g_down = product("bsf,bsd->fd", activated, d_next)
    d_activated = product("bsd,fd->bsf", d_next, w_down).astype(jnp.bfloat16)
    gelu_pull = jax.vjp(gelu_tanh, pre_act.astype(jnp.float32))[1]
    d_pre = gelu_pull(d_activated.astype(jnp.float32))[0].astype(jnp.bfloat16)
    g_up = product("bsd,bsf->df", normed2, d_pre)
    d_normed2 = product("bsf,df->bsd", d_pre, w_up).astype(jnp.bfloat16)
    hidden_pull = jax.vjp(rms_norm, hidden.astype(jnp.float32))[1]
    d_hidden = (d_next.astype(jnp.float32) + hidden_pull(d_normed2.astype(jnp.float32))[0]).astype(jnp.bfloat16)
    g_proj = product("bsd,bse->de", mixed, d_hidden)
    d_mixed = product("bse,de->bsd", d_hidden, w_proj).astype(jnp.bfloat16).reshape(batch, seq_len, heads, head_dim)
    d_probs = product("bqhd,bkhd->bhqk", d_mixed, value).astype(jnp.bfloat16).astype(jnp.float32)
    d_value = product("bhqk,bqhd->bkhd", probs, d_mixed).astype(jnp.bfloat16).reshape(batch, seq_len, width)
    probs_f32 = probs.astype(jnp.float32)
    row_dot = jnp.sum(d_probs * probs_f32, axis=-1, keepdims=True)
    d_scores = (probs_f32 * (d_probs - row_dot) * head_dim ** -0.5).astype(jnp.bfloat16)
    d_query = product("bhqk,bkhd->bqhd", d_scores, key_act).astype(jnp.bfloat16).reshape(batch, seq_len, width)
    d_key = product("bhqk,bqhd->bkhd", d_scores, query).astype(jnp.bfloat16).reshape(batch, seq_len, width)
    g_query = product("bsd,bse->de", normed, d_query)
    g_key = product("bsd,bse->de", normed, d_key)
    g_value = product("bsd,bse->de", normed, d_value)
    d_normed = (product("bse,de->bsd", d_query, w_query) + product("bse,de->bsd", d_key, w_key)
                + product("bse,de->bsd", d_value, w_value)).astype(jnp.bfloat16)
    input_pull = jax.vjp(rms_norm, x_act.astype(jnp.float32))[1]
    d_input = (d_hidden.astype(jnp.float32) + input_pull(d_normed.astype(jnp.float32))[0]).astype(jnp.bfloat16)
    return d_input, (g_query, g_key, g_value, g_proj), g_up, g_down


def solution(mesh):
    def local_step(x_init, cot_out, w_query, w_key, w_value, w_proj, w_up, w_down):
        heads = x_init.shape[-1] // HEAD_DIM
        layers = w_query.shape[0]
        x_act = x_init
        kept_all = []
        for layer in range(layers):
            x_act, kept = layer_forward(x_act, w_query[layer], w_key[layer], w_value[layer], w_proj[layer], w_up, w_down, heads)
            kept_all.append(kept)
        d_act = cot_out
        g_up = jnp.zeros(w_up.shape, jnp.float32)
        g_down = jnp.zeros(w_down.shape, jnp.float32)
        attn_grads = []
        for layer in reversed(range(layers)):
            d_act, attn_part, up_part, down_part = layer_backward(
                d_act, kept_all[layer], w_query[layer], w_key[layer], w_value[layer], w_proj[layer], w_up, w_down)
            attn_part, up_part, down_part = lax.psum((attn_part, up_part, down_part), "data")
            attn_grads.append(attn_part)
            g_up = g_up + up_part
            g_down = g_down + down_part
        attn_grads = attn_grads[::-1]
        g_query = jnp.stack([part[0] for part in attn_grads])
        g_key = jnp.stack([part[1] for part in attn_grads])
        g_value = jnp.stack([part[2] for part in attn_grads])
        g_proj = jnp.stack([part[3] for part in attn_grads])
        return g_query, g_key, g_value, g_proj, g_up, g_down, d_act

    data_spec = P("data")
    full_spec = P()
    in_specs = (data_spec, data_spec, full_spec, full_spec, full_spec, full_spec, full_spec, full_spec)
    out_specs = (full_spec, full_spec, full_spec, full_spec, full_spec, full_spec, data_spec)
    return jax.shard_map(local_step, mesh=mesh, in_specs=in_specs, out_specs=out_specs, check_vma=False)
```

profile of v0, /device:TPU:0, one launch (start us, length us, event | category | flops | bytes accessed | tf_op | source)
XLA Modules:
  0.0 1491.0 jit_solution(1553701749420516945)
XLA Ops:
  9.9 5.9 fusion.135
  18.8 6.7 fusion.132
  29.5 5.9 fusion.129
  39.3 10.7 fusion.230
  50.0 6.8 divide_convert_fusion.1
  68.2 11.9 fusion.64
  80.1 14.0 fusion.93
  113.3 11.5 fusion.231
  124.9 6.9 divide_convert_fusion
  140.6 11.7 fusion.67
  152.2 22.6 %fusion.10 = bf16[4,256,4096]{2,1,0:T(8,128)(2,1)} fusion(bf16[4,256,4096]{2,1,0:T(8,128)(2,1)} %fusion.67, bf16[4,256,1024]{2,1,0:T(8,128)(2,1)S(1)} %copy-done.20, bf16[4096,1024]{1,0:T(8,128)(2,1)} %param.15), kind=kOutput, calls=%fused_computation.28 | convolution fusion | flops 8686403584 | bytes 27262976 | tf_op jit(solution)/shard_map/bsd,fd->bsf/dot_general | solution.py:19
  174.8 14.3 fusion.84
  201.5 7.5 convolution_convert_fusion.3
  209.0 5.8 convolution_convert_fusion.1
  214.8 16.2 %fusion.159 = bf16[4,16,64,256]{3,2,1,0:T(8,128)(2,1)} fusion(bf16[4,256,16,64]{1,3,2,0:T(8,128)(2,1)} %bitcast.251, bf16[4,16,256,256]{2,3,1,0:T(8,128)(2,1)} %copy-done.1, bf16[4,16,256,256]{2,3,1,0:T(8,128)(2,1)} %convolution_convert_fusion.1), kind=kOutput, calls=%fused_computation.195 | convolution fusion | flops 575684864 | bytes 20971520 | tf_op jit(solution)/shard_map/bhqk,bkhd->bqhd/dot_general | solution.py:19
  231.0 18.4 %fusion.160 = bf16[4,16,64,256]{3,2,1,0:T(8,128)(2,1)} fusion(bf16[4,256,16,64]{1,3,2,0:T(8,128)(2,1)} %bitcast.253, bf16[4,16,256,256]{2,3,1,0:T(8,128)(2,1)} %copy-done.1, bf16[4,16,256,256]{2,3,1,0:T(8,128)(2,1)} %convolution_convert_fusion.1), kind=kOutput, calls=%fused_computation.196 | convolution fusion | flops 575684864 | bytes 20971520 | tf_op jit(solution)/shard_map/bhqk,bqhd->bkhd/dot_general | solution.py:19
  249.4 6.4 convolution_bitcast_fusion.6
  265.5 15.5 %fusion.187 = f32[1024,4096,1]{1,0,2:T(8,128)} fusion(bf16[4,256,4096]{2,1,0:T(8,128)(2,1)} %fusion.10, bf16[4,256,1024]{2,1,0:T(8,128)(2,1)S(1)} %copy-done.29, f32[4,256]{1,0:T(4,128)S(1)} %fusion.209), kind=kOutput, calls=%fused_computation.219 | convolution fusion | flops 8593080320 | bytes 27267072 | tf_op jit(solution)/shard_map/bsd,bsf->df/dot_general | solution.py:19
  289.9 23.4 %fusion.15 = bf16[4,256,4096]{2,1,0:T(8,128)(2,1)} fusion(bf16[4,256,4096]{2,1,0:T(8,128)(2,1)} %fusion.64, bf16[4,256,1024]{2,1,0:T(8,128)(2,1)S(1)} %fusion.77, bf16[4096,1024]{1,0:T(8,128)(2,1)} %param.15), kind=kOutput, calls=%fused_computation.33 | convolution fusion | flops 8686403584 | bytes 27262976 | tf_op jit(solution)/shard_map/bsd,fd->bsf/dot_general | solution.py:19
  313.3 14.1 fusion.92
  340.0 7.5 convolution_convert_fusion.2
  347.5 5.8 convolution_convert_fusion
  353.3 16.3 %fusion.157 = bf16[4,16,64,256]{3,2,1,0:T(8,128)(2,1)} fusion(bf16[4,256,16,64]{1,3,2,0:T(8,128)(2,1)} %bitcast.249, bf16[4,16,256,256]{2,3,1,0:T(8,128)(2,1)} %copy-done, bf16[4,16,256,256]{2,3,1,0:T(8,128)(2,1)} %convolution_convert_fusion), kind=kOutput, calls=%fused_computation.193 | convolution fusion | flops 575684864 | bytes 20971520 | tf_op jit(solution)/shard_map/bhqk,bkhd->bqhd/dot_general | solution.py:19
  369.6 18.4 %fusion.158 = bf16[4,16,64,256]{3,2,1,0:T(8,128)(2,1)} fusion(bf16[4,256,16,64]{1,3,2,0:T(8,128)(2,1)} %bitcast.247, bf16[4,16,256,256]{2,3,1,0:T(8,128)(2,1)} %copy-done, bf16[4,16,256,256]{2,3,1,0:T(8,128)(2,1)} %convolution_convert_fusion), kind=kOutput, calls=%fused_computation.194 | convolution fusion | flops 575684864 | bytes 20971520 | tf_op jit(solution)/shard_map/bhqk,bqhd->bkhd/dot_general | solution.py:19
  388.0 18.4 %fusion.38 = f32[4096,1024,1]{1,0,2:T(8,128)} fusion(bf16[4,256,1024]{2,1,0:T(8,128)(2,1)S(1)} %copy-done.21, bf16[4,256,4096]{2,1,0:T(8,128)(2,1)} %fusion.67), kind=kOutput, calls=%fused_computation.60 | convolution fusion | flops 8631877632 | bytes 27262976 | tf_op jit(solution)/shard_map/bsf,bsd->fd/dot_general | solution.py:19
  406.4 19.0 %bitcast_add_fusion.1 = f32[1024,4096]{1,0:T(8,128)} fusion(f32[1024,4096,1]{1,0,2:T(8,128)} %fusion.187, bf16[4,256,4096]{2,1,0:T(8,128)(2,1)} %fusion.15, bf16[4,256,1024]{2,1,0:T(8,128)(2,1)S(1)} %copy-done.24, f32[4,256]{1,0:T(4,128)S(1)} %copy-done.37), kind=kOutput, calls=%fused_computation.49 | convolution fusion | flops 8597274624 | bytes 44044288 | tf_op jit(solution)/shard_map/bsd,bsf->df/dot_general | solution.py:19
  439.5 21.3 %bitcast_add_fusion = f32[4096,1024]{1,0:T(8,128)} fusion(f32[4096,1024,1]{1,0,2:T(8,128)} %fusion.38, bf16[4,256,1024]{2,1,0:T(8,128)(2,1)S(1)} %copy-done.9, bf16[4,256,4096]{2,1,0:T(8,128)(2,1)} %fusion.64), kind=kOutput, calls=%fused_computation.48 | convolution fusion | flops 8636071936 | bytes 44040192 | tf_op jit(solution)/shard_map/bsf,bsd->fd/dot_general | solution.py:19
  473.9 966.4 %all-reduce.3.cloned.1.call-done = (f32[1,1024,1024]{2,1,0:T(8,128)}, f32[1,1024,1024]{2,1,0:T(8,128)}, f32[1,1024,1024]{2,1,0:T(8,128)}, f32[1,1024,1024]{2,1,0...) async-done(((f32[1,1024,1024]{2,1,0:T(8,128)}, ...) | async-done | bytes 67108880 | tf_op jit(solution)/shard_map/psum | solution.py:91
  1440.3 13.4 pad_maximum_fusion
  1455.5 9.1 pad_maximum_fusion.2
  1464.5 13.0 copy.145
  1477.8 6.2 copy.146
  (185 shorter events, 125.2 us)
Async XLA Ops:
  7.2 1433.1 %all-reduce.3.cloned.1.call-start = ((), (), s32[]{:S(2)}) async-start(), calls=%async_computation | async-start | bytes 134217728 | tf_op jit(solution)/shard_map/psum | solution.py:91
  9.9 19.6 %copy-start.34 = (f32[4,256]{1,0:T(4,128)}, f32[4,256]{1,0:T(4,128)S(1)}, u32[]{:S(2)}) copy-start(f32[4,256]{1,0:T(4,128)S(1)} %fusion.206) | copy-start | bytes 12292
  18.8 38.0 %copy-start.2 = (bf16[4,256,1024]{1,2,0:T(8,128)(2,1)}, bf16[4,256,1024]{1,2,0:T(8,128)(2,1)S(1)}, u32[]{:S(2)}) copy-start(bf16[4,256,1024]{1,2,0:T(8,128)(2,1)S(1)} %copy.65) | copy-start | bytes 6291460
  56.9 11.3 slice-start.6
  61.1 19.0 %slice-start.4 = ((s8[8388608]{0:T(1024)(128)(4,1)}), s8[4194304]{0:T(1024)(128)(4,1)S(1)}, s32[]{:S(2)}) async-start(s8[8388608]{0:T(1024)(128)(4,1)} %bitcast.258), calls=%async_computation.5 | async-start | bytes 8388608
  66.9 13.1 copy-start.22
  68.2 11.9 slice-start.5
  80.1 14.1 copy-start.50
  113.3 18.5 %copy-start.4 = (bf16[4,256,1024]{1,2,0:T(8,128)(2,1)}, bf16[4,256,1024]{1,2,0:T(8,128)(2,1)S(1)}, u32[]{:S(2)}) copy-start(bf16[4,256,1024]{1,2,0:T(8,128)(2,1)S(1)} %copy.68) | copy-start | bytes 6291460
  131.9 8.7 slice-start.8
  140.5 48.6 %copy-start.28 = (bf16[4,256,1024]{2,1,0:T(8,128)(2,1)}, bf16[4,256,1024]{2,1,0:T(8,128)(2,1)S(1)}, u32[]{:S(2)}) copy-start(bf16[4,256,1024]{2,1,0:T(8,128)(2,1)S(1)} %get-tuple-element.26) | copy-start | bytes 6291460
  140.6 11.7 copy-start.20
  201.5 7.5 copy-start.5
  231.0 18.4 %copy-start.27 = (bf16[4,256,1024]{2,1,0:T(8,128)(2,1)S(1)}, bf16[4,256,1024]{2,1,0:T(8,128)(2,1)}, u32[]{:S(2)}) copy-start(bf16[4,256,1024]{2,1,0:T(8,128)(2,1)} %copy-done.25) | copy-start | bytes 6291460
  265.5 15.5 %copy-start.16 = (bf16[4,16,64,256]{3,2,1,0:T(8,128)(2,1)S(1)}, bf16[4,16,64,256]{3,2,1,0:T(8,128)(2,1)}, u32[]{:S(2)}) copy-start(bf16[4,16,64,256]{3,2,1,0:T(8,128)(2,1)} %convolution_convert_fusion.3) | copy-start | bytes 6291460
  289.8 37.5 %copy-start.8 = (bf16[4,256,1024]{2,1,0:T(8,128)(2,1)}, bf16[4,256,1024]{2,1,0:T(8,128)(2,1)S(1)}, u32[]{:S(2)}) copy-start(bf16[4,256,1024]{2,1,0:T(8,128)(2,1)S(1)} %fusion.77) | copy-start | bytes 6291460
  289.9 23.4 %copy-start.23 = (bf16[4,256,1024]{2,1,0:T(8,128)(2,1)S(1)}, bf16[4,256,1024]{2,1,0:T(8,128)(2,1)}, u32[]{:S(2)}) copy-start(bf16[4,256,1024]{2,1,0:T(8,128)(2,1)} %copy-done.22) | copy-start | bytes 6291460
  313.2 14.1 copy-start.39
  313.2 14.1 copy-start.37
  340.0 7.5 copy-start.3
  369.6 18.4 %copy-start.21 = (bf16[4,256,1024]{2,1,0:T(8,128)(2,1)S(1)}, bf16[4,256,1024]{2,1,0:T(8,128)(2,1)}, u32[]{:S(2)}) copy-start(bf16[4,256,1024]{2,1,0:T(8,128)(2,1)} %param.9) | copy-start | bytes 6291460
  387.9 18.4 %copy-start.24 = (bf16[4,256,1024]{2,1,0:T(8,128)(2,1)S(1)}, bf16[4,256,1024]{2,1,0:T(8,128)(2,1)}, u32[]{:S(2)}) copy-start(bf16[4,256,1024]{2,1,0:T(8,128)(2,1)} %copy-done.22) | copy-start | bytes 6291460
  406.4 19.0 %copy-start.13 = (bf16[4,256,1024]{2,1,0:T(8,128)(2,1)S(1)}, bf16[4,256,1024]{2,1,0:T(8,128)(2,1)}, u32[]{:S(2)}) copy-start(bf16[4,256,1024]{2,1,0:T(8,128)(2,1)} %param.8) | copy-start | bytes 6291460
  406.4 19.0 %copy-start.35 = (f32[4,256]{1,0:T(4,128)S(1)}, f32[4,256]{1,0:T(4,128)}, u32[]{:S(2)}) copy-start(f32[4,256]{1,0:T(4,128)} %copy-done.34) | copy-start | bytes 12292
  406.4 19.0 %copy-start.55 = (bf16[4,16,64,256]{3,2,1,0:T(8,128)(2,1)S(1)}, bf16[4,16,64,256]{3,2,1,0:T(8,128)(2,1)}, u32[]{:S(2)}) copy-start(bf16[4,16,64,256]{3,2,1,0:T(8,128)(2,1)} %fusion.157) | copy-start | bytes 6291460
  1440.2 13.4 copy-start.17
  1440.3 13.4 copy-start.18
  1440.3 15.2 %copy-start.19 = (f32[1,1024,1024]{2,1,0:T(8,128)S(1)}, f32[1,1024,1024]{2,1,0:T(8,128)}, u32[]{:S(2)}) copy-start(f32[1,1024,1024]{2,1,0:T(8,128)} %get-tuple-element.13) | copy-start | bytes 12582916
  1455.5 22.1 %slice-start = ((s8[16777216]{0:T(1024)(128)(4,1)}), s8[4194304]{0:T(1024)(128)(4,1)S(1)}, s32[]{:S(2)}) async-start(s8[16777216]{0:T(1024)(128)(4,1)} %bitcast.240), calls=%async_computation.1 | async-start | bytes 8388608
  1455.5 22.1 %slice-start.1 = ((s8[16777216]{0:T(1024)(128)(4,1)}), s8[4194304]{0:T(1024)(128)(4,1)S(1)}, s32[]{:S(2)}) async-start(s8[16777216]{0:T(1024)(128)(4,1)} %bitcast.240), calls=%async_computation.2 | async-start | bytes 8388608
  1464.5 13.0 slice-start.2
  1464.5 13.2 slice-start.3
  (37 other events, 143.5 us)
Sparse Core Ops, SparseCore 0:
  461.0 979.2 all-reduce.2
where the time goes:
time: 1490 us
  waiting for transfers between devices  966 us (65%)
  matrix products  408 us (27%)
  local copies, waits for them, and re-layouts  56.6 us (4%)
  other arithmetic  44.7 us (3%)
  between operations  15 us (1%)
    psum x1, waiting for transfers between devices, local_step(): lax.psum((attn_part, up_part, down_part), 'data')  966 us
    dot_general x45, matrix products, product(): return jnp.einsum(subscripts, lhs, rhs, preferred_element_type=jnp.float32)  386 us
    unnamed x138, local copies, waits for them, and re-layouts  30.7 us
  transfers between devices with their start and end apart: 1, of which 1 were waited for; matrix products, arithmetic and copies ran while one was open for 1% of the time, Pallas kernels for 0%

commit v1 on v0

--- a/solution.py
+++ b/solution.py
@@ -1,6 +1,10 @@
+import functools
+
 import jax
 import jax.numpy as jnp
 from jax import lax
+from jax.experimental import pallas as pl
+from jax.experimental.pallas import tpu as pltpu
 from jax.sharding import PartitionSpec as P
 
 EPS = 1e-6
@@ -45,15 +49,12 @@
     x_act, normed, query, key_act, value, probs, mixed, hidden, normed2, pre_act, activated = kept
     batch, seq_len, heads, head_dim = query.shape
     width = heads * head_dim
-    g_down = product("bsf,bsd->fd", activated, d_next)
     d_activated = product("bsd,fd->bsf", d_next, w_down).astype(jnp.bfloat16)
     gelu_pull = jax.vjp(gelu_tanh, pre_act.astype(jnp.float32))[1]
     d_pre = gelu_pull(d_activated.astype(jnp.float32))[0].astype(jnp.bfloat16)
-    g_up = product("bsd,bsf->df", normed2, d_pre)
     d_normed2 = product("bsf,df->bsd", d_pre, w_up).astype(jnp.bfloat16)
     hidden_pull = jax.vjp(rms_norm, hidden.astype(jnp.float32))[1]
     d_hidden = (d_next.astype(jnp.float32) + hidden_pull(d_normed2.astype(jnp.float32))[0]).astype(jnp.bfloat16)
-    g_proj = product("bsd,bse->de", mixed, d_hidden)
     d_mixed = product("bse,de->bsd", d_hidden, w_proj).astype(jnp.bfloat16).reshape(batch, seq_len, heads, head_dim)
     d_probs = product("bqhd,bkhd->bhqk", d_mixed, value).astype(jnp.bfloat16).astype(jnp.float32)
     d_value = product("bhqk,bqhd->bkhd", probs, d_mixed).astype(jnp.bfloat16).reshape(batch, seq_len, width)
@@ -62,42 +63,423 @@
     d_scores = (probs_f32 * (d_probs - row_dot) * head_dim ** -0.5).astype(jnp.bfloat16)
     d_query = product("bhqk,bkhd->bqhd", d_scores, key_act).astype(jnp.bfloat16).reshape(batch, seq_len, width)
     d_key = product("bhqk,bqhd->bkhd", d_scores, query).astype(jnp.bfloat16).reshape(batch, seq_len, width)
-    g_query = product("bsd,bse->de", normed, d_query)
-    g_key = product("bsd,bse->de", normed, d_key)
-    g_value = product("bsd,bse->de", normed, d_value)
     d_normed = (product("bse,de->bsd", d_query, w_query) + product("bse,de->bsd", d_key, w_key)
                 + product("bse,de->bsd", d_value, w_value)).astype(jnp.bfloat16)
     input_pull = jax.vjp(rms_norm, x_act.astype(jnp.float32))[1]
     d_input = (d_hidden.astype(jnp.float32) + input_pull(d_normed.astype(jnp.float32))[0]).astype(jnp.bfloat16)
-    return d_input, (g_query, g_key, g_value, g_proj), g_up, g_down
+    attn = (normed, d_query, d_key, d_value, mixed, d_hidden)
+    mlp = (normed2, d_pre, activated, d_next)
+    flat = lambda arr: arr.reshape(batch * seq_len, -1)
+    return d_input, tuple(map(flat, attn)), tuple(map(flat, mlp))
+
+
+MESH = pl.DeviceIdType.MESH
+LANES = 1024
+SET_ROWS = 128
+CORE_ROWS = 2 * SET_ROWS
+TILE_ROWS = 2 * CORE_ROWS
+OWN_SLOTS = 8
+AG_SLOTS = 10
+TYPES = {
+    "p1": (0, 0, 80, "xyz"),
+    "q1": (0, 80, 48, "zxy"),
+    "p2": (1, 128, 80, "yxz"),
+    "q2": (1, 208, 48, "zyx"),
+}
+WRITE_AT = 11
+
+
+def stage_list():
+    stages = []
+    for name, (_, _, _, order) in TYPES.items():
+        if order[2] == "z":
+            plan = [("rs1", 1), ("rs2", 2), ("rsz", 3), ("agz", 6), ("ag2", 9), ("ag1", 10)]
+        else:
+            plan = [("rsz", 1), ("rs1", 4), ("rs2", 5), ("ag2", 6), ("ag1", 7), ("agz", 8)]
+        for kind, at in plan:
+            if kind in ("rsz", "agz"):
+                for step in range(3):
+                    for way in (0, 1):
+                        stages.append((name, kind, step, way, at + step))
+            else:
+                stages.append((name, kind, 0, 0, at))
+    return stages
+
+
+STAGES = stage_list()
+
+
+def piece_shape(name, kind):
+    rows, order = TYPES[name][2], TYPES[name][3]
+    if order[2] == "z":
+        return {"rs1": (rows, 512), "rs2": (rows, 256), "rsz": (rows // 2, 128)}[kind]
+    return {"rsz": (rows // 2, 512), "rs1": (rows // 2, 256), "rs2": (rows // 2, 128)}[kind]
+
+
+def reduce_kernel(groups, chunks, n_in, n_out, *refs):
+    ins, outs, scratch = refs[:n_in], refs[n_in:n_in + n_out], refs[n_in + n_out:]
+    (lhs_buf, rhs_buf, own, part, part_in, gath), scratch = scratch[:6], scratch[6:]
+    land_keys = [key for key, st in enumerate(STAGES) if st[1].startswith("rs")]
+    landing = dict(zip(land_keys, scratch[:len(land_keys)]))
+    load_sem, send_sem, recv_sem, pair_send, pair_recv, out_sem, out_send, out_recv, credit = scratch[len(land_keys):]
+
+    me = lax.axis_index("data")
+    core = lax.rem(me, 2)
+    coord = {"x": lax.rem(lax.div(me, 2), 2), "y": lax.rem(lax.div(me, 4), 2)}
+    z = lax.div(me, 8)
+    partner = me + 1 - 2 * core
+    near = {"x": me + 2 - 4 * coord["x"], "y": me + 4 - 8 * coord["y"]}
+    up_ok, down_ok = z < 3, z > 0
+    peers = [(partner, 0, None), (near["x"], 1, None), (near["y"], 2, None), (me + 8, 3, up_ok), (me - 8, 4, down_ok)]
+
+    def guarded(cond, fn):
+        if cond is None:
+            fn()
+        else:
+            pl.when(cond)(fn)
+
+    barrier = pltpu.get_barrier_semaphore()
+    for dev, _, cond in peers:
+        guarded(cond, lambda dev=dev: pl.semaphore_signal(barrier, inc=1, device_id=(dev,), device_id_type=MESH))
+    inner = jnp.logical_and(up_ok, down_ok)
+    guarded(inner, lambda: pl.semaphore_wait(barrier, 5))
+    guarded(jnp.logical_not(inner), lambda: pl.semaphore_wait(barrier, 4))
+
+    def region(name, kind, which):
+        _, row, rows, order = TYPES[name]
+        if order[2] == "z":
+            h1, h2 = coord[order[0]], coord[order[1]]
+            if kind == "1":
+                return pl.ds(row, rows), pl.ds(pl.multiple_of(512 * which, 128), 512)
+            if kind == "2":
+                return pl.ds(row, rows), pl.ds(pl.multiple_of(512 * h1 + 256 * which, 128), 256)
+            first = pl.multiple_of(row + (rows // 2) * lax.div(which, 2), 8)
+            lane = pl.multiple_of(512 * h1 + 256 * h2 + 128 * lax.rem(which, 2), 128)
+            return pl.ds(first, rows // 2), pl.ds(lane, 128)
+        h1 = coord[order[1]]
+        if kind == "z":
+            first = pl.multiple_of(row + (rows // 2) * lax.div(which, 2), 8)
+            return pl.ds(first, rows // 2), pl.ds(pl.multiple_of(512 * lax.rem(which, 2), 128), 512)
+        first = pl.multiple_of(row + (rows // 2) * lax.div(z, 2), 8)
+        if kind == "1":
+            return pl.ds(first, rows // 2), pl.ds(pl.multiple_of(512 * lax.rem(z, 2) + 256 * which, 128), 256)
+        lane = pl.multiple_of(512 * lax.rem(z, 2) + 256 * h1 + 128 * which, 128)
+        return pl.ds(first, rows // 2), pl.ds(lane, 128)
+
+    def exchange_axis(name, kind):
+        order = TYPES[name][3]
+        dims = order[:2] if order[2] == "z" else order[1:]
+        return dims[int(kind) - 1]
+
+    def plan(key, chunk, parity):
+        name, kind, step, way, _ = STAGES[key]
+        mine, slot = lax.rem(chunk, OWN_SLOTS), lax.rem(chunk, AG_SLOTS)
+        if kind in ("rs1", "rs2"):
+            axis = exchange_axis(name, kind[2])
+            src, keep = region(name, kind[2], 1 - coord[axis]), region(name, kind[2], coord[axis])
+            dev, send_ok, recv_ok = near[axis], None, None
+            sent = own.at[mine, src[0], src[1]]
+        elif kind in ("ag1", "ag2"):
+            axis = exchange_axis(name, kind[2])
+            src = keep = region(name, kind[2], coord[axis])
+            dev, send_ok, recv_ok = near[axis], None, None
+            sent = gath.at[slot, src[0], src[1]]
+        elif kind == "rsz":
+            if way:
+                dev, k_send, k_keep = me + 8, z + 3 - step, z + 2 - step
+                send_ok, recv_ok = k_send <= 3, jnp.logical_and(k_keep <= 3, down_ok)
+            else:
+                dev, k_send, k_keep = me - 8, z - 3 + step, z - 2 + step
+                send_ok, recv_ok = k_send >= 0, jnp.logical_and(k_keep >= 0, up_ok)
+            src, keep = region(name, "z", k_send), region(name, "z", k_keep)
+            sent = own.at[mine, src[0], src[1]]
+        else:
+            if way:
+                dev, k_send, k_keep = me + 8, z - step, z - 1 - step
+                send_ok, recv_ok = jnp.logical_and(k_send >= 0, up_ok), k_keep >= 0
+            else:
+                dev, k_send, k_keep = me - 8, z + step, z + 1 + step
+                send_ok, recv_ok = jnp.logical_and(k_send <= 3, down_ok), k_keep <= 3
+            src, keep = region(name, "z", k_send), region(name, "z", k_keep)
+            sent = gath.at[slot, src[0], src[1]]
+        sems = dict(send_sem=send_sem.at[key], recv_sem=recv_sem.at[key, parity], device_id=(dev,), device_id_type=MESH)
+        if kind.startswith("rs"):
+            target = landing[key].at[parity]
+            send = lambda: pltpu.make_async_remote_copy(src_ref=sent, dst_ref=target, **sems)
+            recv = lambda: pltpu.make_async_remote_copy(
+                src_ref=own.at[mine, keep[0], keep[1]], dst_ref=target, **sems)
+
+            def arrive():
+                own[mine, keep[0], keep[1]] += landing[key][parity]
+        else:
+            send = lambda: pltpu.make_async_remote_copy(src_ref=sent, dst_ref=sent, **sems)
+            recv = lambda: pltpu.make_async_remote_copy(
+                src_ref=gath.at[slot, keep[0], keep[1]], dst_ref=gath.at[slot, keep[0], keep[1]], **sems)
+            arrive = None
+        return send, recv, send_ok, recv_ok, arrive
+
+    def finish(name, chunk):
+        order = TYPES[name][3]
+        reg = region(name, "z", z) if order[2] == "z" else region(name, "2", coord[order[2]])
+        gath[lax.rem(chunk, AG_SLOTS), reg[0], reg[1]] = own[lax.rem(chunk, OWN_SLOTS), reg[0], reg[1]]
+
+    def valid(chunk):
+        return jnp.logical_and(chunk >= 0, chunk < chunks)
+
+    def set_rows(half):
+        return pl.ds(half * SET_ROWS, SET_ROWS)
+
+    def pair_copy(half, parity):
+        return pltpu.make_async_remote_copy(
+            src_ref=part.at[parity, set_rows(half)], dst_ref=part_in.at[parity, set_rows(half)],
+            send_sem=pair_send.at[half], recv_sem=pair_recv.at[half, parity], device_id=(partner,), device_id_type=MESH)
+
+    def out_copies(half, group, local, whose):
+        out, layer = group["out"]
+        ref = outs[out] if layer is None else outs[out].at[layer]
+        rows, cols = group["place"](local)
+        first = pl.multiple_of(rows + CORE_ROWS * whose + half * SET_ROWS, SET_ROWS)
+        return ref.at[pl.ds(first, SET_ROWS), pl.ds(pl.multiple_of(cols, 128), LANES)]
+
+    def write_copies(half, chunk, dest):
+        slot = lax.rem(chunk, AG_SLOTS)
+        src = gath.at[slot, set_rows(half)]
+        here = pltpu.make_async_copy(src, dest, out_sem.at[half])
+        there = pltpu.make_async_remote_copy(
+            src_ref=src, dst_ref=dest, send_sem=out_send.at[half], recv_sem=out_recv.at[half, lax.rem(chunk, 2)],
+            device_id=(partner,), device_id_type=MESH)
+        return here, there
+
+    def load_copies(group, local, slot):
+        rows, cols = group["place"](local)
+        copies = []
+        for app, (lhs, rhs) in enumerate(zip(group["lhs"], group["rhs"])):
+            for whose in (0, 1):
+                first = rows + CORE_ROWS * (core if whose == 0 else 1 - core)
+                copies.append(pltpu.make_async_copy(
+                    ins[lhs].at[:, pl.ds(pl.multiple_of(first, CORE_ROWS), CORE_ROWS)],
+                    lhs_buf.at[slot, app, whose], load_sem.at[slot, app, whose]))
+            copies.append(pltpu.make_async_copy(
+                ins[rhs].at[:, pl.ds(pl.multiple_of(cols, 128), LANES)], rhs_buf.at[slot, app], load_sem.at[slot, app, 2]))
+        return copies
+
+    def for_group(chunk, fn):
+        for group in groups:
+            inside = jnp.logical_and(chunk >= group["start"], chunk < group["start"] + group["count"])
+            pl.when(inside)(functools.partial(fn, group, chunk - group["start"]))
+
+    def two_apps(chunk):
+        flags = [jnp.logical_and(chunk >= g["start"], chunk < g["start"] + g["count"]) for g in groups if len(g["lhs"]) == 2]
+        return functools.reduce(jnp.logical_or, flags)
+
+    def start_load(chunk):
+        def go(group, local):
+            for copy in load_copies(group, local, lax.rem(chunk, 2)):
+                copy.start()
+        for_group(chunk, go)
+
+    def wait_load(chunk):
+        slot = lax.rem(chunk, 2)
+        any_two = next(g for g in groups if len(g["lhs"]) == 2)
+        copies = load_copies(any_two, 0, slot)
+        for copy in copies[:3]:
+            copy.wait()
+
+        @pl.when(two_apps(chunk))
+        def _():
+            for copy in copies[3:]:
+                copy.wait()
+
+    def tile(chunk):
+        slot, mine, parity = lax.rem(chunk, 2), lax.rem(chunk, OWN_SLOTS), lax.rem(chunk, 2)
+
+        def product(app, whose):
+            return lax.dot_general(lhs_buf[slot, app, whose], rhs_buf[slot, app], (((0,), (0,)), ((), ())),
+                                   preferred_element_type=jnp.float32)
+
+        own[mine] = product(0, 0)
+        part[parity] = product(0, 1)
+
+        @pl.when(two_apps(chunk))
+        def _():
+            own[mine] += product(1, 0)
+            part[parity] += product(1, 1)
+
+    last = chunks + WRITE_AT
+
+    def section(half, step):
+        before = lax.rem(step + 1, 2)
+        now = lax.rem(step, 2)
+
+        @pl.when(valid(step - 1))
+        def _():
+            copy = pair_copy(half, before)
+            copy.wait_send()
+            copy.wait_recv()
+            mine = lax.rem(step - 1, OWN_SLOTS)
+            own[mine, set_rows(half)] += part_in[before, set_rows(half)]
+
+        names = [name for name in TYPES if TYPES[name][0] == half]
+        keys = [key for key, st in enumerate(STAGES) if st[0] in names]
+        finals = {name: max(st[4] for st in STAGES if st[0] == name and st[1].startswith("rs")) for name in names}
+        for key in keys:
+            name, at = STAGES[key][0], STAGES[key][4]
+            chunk = step - 1 - at
+
+            @pl.when(valid(chunk))
+            def _(key=key, chunk=chunk):
+                send, recv, send_ok, recv_ok, arrive = plan(key, chunk, before)
+
+                def arrived():
+                    recv().wait_recv()
+                    if arrive is not None:
+                        arrive()
+                guarded(recv_ok, arrived)
+                guarded(send_ok, lambda: send().wait_send())
+        for name in names:
+            chunk = step - 1 - finals[name]
+            pl.when(valid(chunk))(functools.partial(finish, name, chunk))
+
+        done = step - 1 - WRITE_AT
+
+        @pl.when(valid(done))
+        def _():
+            here, there = write_copies(half, done, out_copies(half, groups[0], 0, 0))
+            here.wait()
+            there.wait_send()
+            there.wait_recv()
+
+        @pl.when(step < last)
+        def _():
+            for dev, way, cond in peers:
+                to = way if way < 3 else 7 - way
+                guarded(cond, lambda dev=dev, to=to: pl.semaphore_signal(
+                    credit.at[half, to], inc=1, device_id=(dev,), device_id_type=MESH))
+
+        @pl.when(step > 0)
+        def _():
+            for dev, way, cond in peers:
+                guarded(cond, lambda way=way: pl.semaphore_wait(credit.at[half, way], 1))
+
+        for key in reversed(keys):
+            chunk = step - STAGES[key][4]
+
+            @pl.when(valid(chunk))
+            def _(key=key, chunk=chunk):
+                send, recv, send_ok, recv_ok, arrive = plan(key, chunk, now)
+                guarded(send_ok, lambda: send().start())
+
+        out_chunk = step - WRITE_AT
+
+        @pl.when(valid(out_chunk))
+        def _():
+            def go(group, local):
+                for copy in write_copies(half, out_chunk, out_copies(half, group, local, core)):
+                    copy.start()
+            for_group(out_chunk, go)
+
+    start_load(jnp.int32(0))
+
+    def round_(step, carry):
+        section(0, step)
+
+        @pl.when(valid(step))
+        def _():
+            pl.when(step + 1 < chunks)(lambda: start_load(step + 1))
+            wait_load(step)
+            tile(step)
+            pair_copy(0, lax.rem(step, 2)).start()
+
+        section(1, step)
+
+        @pl.when(valid(step))
+        def _():
+            pair_copy(1, lax.rem(step, 2)).start()
+
+        return carry
+
+    lax.fori_loop(0, last + 1, round_, 0)
+
+
+def reduce_gradients(operands, groups, chunks, out_shapes, tokens, collective_id=0):
+    landing = [pltpu.VMEM((2,) + piece_shape(st[0], st[1]), jnp.float32) for st in STAGES if st[1].startswith("rs")]
+    apps = max(len(g["lhs"]) for g in groups)
+    scratch = [
+        pltpu.VMEM((2, apps, 2, tokens, CORE_ROWS), jnp.bfloat16),
+        pltpu.VMEM((2, apps, tokens, LANES), jnp.bfloat16),
+        pltpu.VMEM((OWN_SLOTS, CORE_ROWS, LANES), jnp.float32),
+        pltpu.VMEM((2, CORE_ROWS, LANES), jnp.float32),
+        pltpu.VMEM((2, CORE_ROWS, LANES), jnp.float32),
+        pltpu.VMEM((AG_SLOTS, CORE_ROWS, LANES), jnp.float32),
+        *landing,
+        pltpu.SemaphoreType.DMA((2, apps, 3)),
+        pltpu.SemaphoreType.DMA((len(STAGES),)),
+        pltpu.SemaphoreType.DMA((len(STAGES), 2)),
+        pltpu.SemaphoreType.DMA((2,)),
+        pltpu.SemaphoreType.DMA((2, 2)),
+        pltpu.SemaphoreType.DMA((2,)),
+        pltpu.SemaphoreType.DMA((2,)),
+        pltpu.SemaphoreType.DMA((2, 2)),
+        pltpu.SemaphoreType.REGULAR((2, 5)),
+    ]
+    flops = sum(2 * g["count"] * len(g["lhs"]) * TILE_ROWS * LANES * tokens for g in groups)
+    return pl.pallas_call(
+        functools.partial(reduce_kernel, groups, chunks, len(operands), len(out_shapes)),
+        out_shape=[jax.ShapeDtypeStruct(shape, jnp.float32) for shape in out_shapes],
+        in_specs=[pl.BlockSpec(memory_space=pl.ANY)] * len(operands),
+        out_specs=[pl.BlockSpec(memory_space=pl.ANY)] * len(out_shapes),
+        scratch_shapes=scratch,
+        compiler_params=pltpu.CompilerParams(
+            collective_id=collective_id, has_side_effects=True, vmem_limit_bytes=60 * 1024 * 1024),
+        cost_estimate=pl.CostEstimate(flops=flops, bytes_accessed=128 * 1024 * 1024, transcendentals=0),
+        name="reduce_gradients",
+    )(*operands)
+
+def gradient_groups(width, ff):
+    groups = []
+
+    def add(count, lhs, rhs, out, place):
+        start = groups[-1]["start"] + groups[-1]["count"] if groups else 0
+        groups.append(dict(start=start, count=count, lhs=lhs, rhs=rhs, out=out, place=place))
+
+    def tall(local):
+        return TILE_ROWS * local, 0
+
+    def wide(local):
+        return TILE_ROWS * lax.rem(local, width // TILE_ROWS), LANES * lax.div(local, width // TILE_ROWS)
+
+    def attention(layer):
+        base = 6 * layer
+        for out in range(3):
+            add(width // TILE_ROWS, [base], [base + 1 + out], (out, layer), tall)
+        add(width // TILE_ROWS, [base + 4], [base + 5], (3, layer), tall)
+
+    attention(1)
+    add(ff // TILE_ROWS, [14, 18], [15, 19], (5, None), tall)
+    add(ff // TILE_ROWS, [12, 16], [13, 17], (4, None), wide)
+    attention(0)
+    return groups, sum(group["count"] for group in groups)
 
 
 def solution(mesh):
     def local_step(x_init, cot_out, w_query, w_key, w_value, w_proj, w_up, w_down):
-        heads = x_init.shape[-1] // HEAD_DIM
-        layers = w_query.shape[0]
+        batch, seq_len, width = x_init.shape
+        heads = width // HEAD_DIM
         x_act = x_init
         kept_all = []
-        for layer in range(layers):
+        for layer in range(2):
             x_act, kept = layer_forward(x_act, w_query[layer], w_key[layer], w_value[layer], w_proj[layer], w_up, w_down, heads)
             kept_all.append(kept)
         d_act = cot_out
-        g_up = jnp.zeros(w_up.shape, jnp.float32)
-        g_down = jnp.zeros(w_down.shape, jnp.float32)
-        attn_grads = []
-        for layer in reversed(range(layers)):
-            d_act, attn_part, up_part, down_part = layer_backward(
+        attn, mlp = [None] * 2, [None] * 2
+        for layer in (1, 0):
+            d_act, attn[layer], mlp[layer] = layer_backward(
                 d_act, kept_all[layer], w_query[layer], w_key[layer], w_value[layer], w_proj[layer], w_up, w_down)
-            attn_part, up_part, down_part = lax.psum((attn_part, up_part, down_part), "data")
-            attn_grads.append(attn_part)
-            g_up = g_up + up_part
-            g_down = g_down + down_part
-        attn_grads = attn_grads[::-1]
-        g_query = jnp.stack([part[0] for part in attn_grads])
-        g_key = jnp.stack([part[1] for part in attn_grads])
-        g_value = jnp.stack([part[2] for part in attn_grads])
-        g_proj = jnp.stack([part[3] for part in attn_grads])
-        return g_query, g_key, g_value, g_proj, g_up, g_down, d_act
+        operands = [*attn[0], *attn[1], *mlp[0], *mlp[1]]
+        groups, chunks = gradient_groups(width, w_up.shape[1])
+        shapes = [w_query.shape, w_key.shape, w_value.shape, w_proj.shape, w_up.shape, w_down.shape]
+        grads = reduce_gradients(operands, groups, chunks, shapes, batch * seq_len)
+        return (*grads, d_act)
 
     data_spec = P("data")
     full_spec = P()

time: 1490 us -> 986 us (0.66)
  waiting for transfers between devices: 966 us -> 0 us
  Pallas kernels: 0 us -> 445 us
  local copies, waits for them, and re-layouts: 56.6 us -> 191 us
  matrix products: 408 us -> 316 us
  other arithmetic: 44.7 us -> 28.2 us
    psum x1 -> x0, waiting for transfers between devices: 966 us -> none  [local_step(): lax.psum((attn_part, up_part, down_part), 'data')]
    pallas_call x0 -> x1, Pallas kernels: none -> 445 us  [reduce_gradients(): pl.pallas_call(functools.partial(reduce_kernel, groups, chunks, len(opera...]
    another operation x0 -> x16, local copies, waits for them, and re-layouts: none -> 97.1 us  [layer_backward(): flat = lambda arr: arr.reshape(batch * seq_len, -1)]
    dot_general x45 -> x33, matrix products: 386 us -> 294 us  [product(): return jnp.einsum(subscripts, lhs, rhs, preferred_element_type=jnp.float32)]
    unnamed x138 -> x126, local copies, waits for them, and re-layouts: 30.7 us -> 66 us
    another operation x2 -> x0, other arithmetic: 22.5 us -> none  [the longest x1 13.4 us: local_step(): g_query = jnp.stack([part[0] for part in attn_grads])]
  transfers between devices with their start and end apart: 1 -> 0, of which waited for: 1 -> 0; matrix products, arithmetic and copies ran while one was open for 1% -> 0% of each run, Pallas kernels for 0% -> 0%
where the time goes in v1:
time: 986 us; the launch traced here: 982 us
  Pallas kernels  445 us (45%)
  matrix products  316 us (32%)
  local copies, waits for them, and re-layouts  191 us (19%)
  other arithmetic  28.2 us (3%)
    pallas_call x1, Pallas kernels, reduce_gradients(): pl.pallas_call(functools.partial(reduce_kernel, groups, chunks, len(opera...  445 us
    dot_general x33, matrix products, product(): return jnp.einsum(subscripts, lhs, rhs, preferred_element_type=jnp.float32)  294 us
    another operation x16, local copies, waits for them, and re-layouts, layer_backward(): flat = lambda arr: arr.reshape(batch * seq_len, -1)  97.1 us
    unnamed x126, local copies, waits for them, and re-layouts  66 us
    sub x2, matrix products, layer_forward(): probs = jax.nn.softmax(scores, axis=-1).astype(jnp.bfloat16)  22.2 us

profile of v1, /device:TPU:0, one launch (start us, length us, event | category | flops | bytes accessed | tf_op | source)
XLA Modules:
  0.0 981.5 jit_solution(17589350106925195219)
XLA Ops:
  13.6 6.6 fusion.126
  34.0 10.8 %fusion.202 = (f32[4,16,256]{2,1,0:T(8,128)S(1)}, f32[4,16,256,256]{2,3,1,0:T(8,128)}) fusion(bf16[4,256,16,64]{1,3,2,0:T(8,128)(2,1)} %bitcast.264, bf16[4,256,16,64]{1,3,2,0:T(8,128)(2,1)} %bitcast.266), kind=kOutput, calls=%fused_computation.224 | convolution fusion | flops 549454080 | bytes 21037056 | tf_op jit(solution)/shard_map/sub | solution.py:35
  44.7 6.8 divide_convert_fusion.1
  69.8 6.5 reshape.209.refs_4_
  76.3 16.7 %fusion.21 = (bf16[4,256,4096]{2,1,0:T(8,128)(2,1)}, bf16[4,256,4096]{2,1,0:T(8,128)(2,1)S(1)}) fusion(bf16[4,256,1024]{2,1,0:T(8,128)(2,1)} %fusion.84, bf16[1024,4096]{1,0:T(8,128)(2,1)} %param.14), kind=kOutput, calls=%fused_computation.39 | convolution fusion | flops 8636071936 | bytes 27262976 | tf_op jit(solution)/shard_map/bsd,df->bsf/dot_general | solution.py:23
  93.0 17.9 %fusion.87 = (f32[4,256]{1,0:T(4,128)S(1)}, bf16[4,256,1024]{2,1,0:T(8,128)(2,1)S(1)}) fusion(bf16[4096,1024]{1,0:T(8,128)(2,1)} %param.15, bf16[4,256,4096]{2,1,0:T(8,128)(2,1)S(1)} %get-tuple-element.36, bf16[4,256,1024]{2,1,0:T(8,128)(2,1)S(1)} %get-tuple-element.22), kind=kOutput, calls=%fused_computation.128 | convolution fusion | flops 8640265216 | bytes 20975616 | tf_op jit(solution)/shard_map/bsf,fd->bsd/dot_general | solution.py:23
  139.0 11.5 %fusion.203 = (f32[4,16,256]{2,1,0:T(8,128)S(1)}, f32[4,16,256,256]{2,3,1,0:T(8,128)}) fusion(bf16[4,256,16,64]{1,3,2,0:T(8,128)(2,1)} %bitcast.270, bf16[4,256,16,64]{1,3,2,0:T(8,128)(2,1)} %bitcast.268), kind=kOutput, calls=%fused_computation.225 | convolution fusion | flops 549454080 | bytes 21037056 | tf_op jit(solution)/shard_map/sub | solution.py:35
  150.5 6.9 divide_convert_fusion
  174.8 6.6 reshape.213.refs_10_
  181.4 18.2 %fusion.29 = (bf16[4,256,4096]{2,1,0:T(8,128)(2,1)}, bf16[4,256,4096]{2,1,0:T(8,128)(2,1)}) fusion(bf16[4,256,1024]{2,1,0:T(8,128)(2,1)} %fusion.77, bf16[1024,4096]{1,0:T(8,128)(2,1)} %param.14), kind=kOutput, calls=%fused_computation.47 | convolution fusion | flops 8636071936 | bytes 27262976 | tf_op jit(solution)/shard_map/bsd,df->bsf/dot_general | solution.py:23
  199.6 22.8 %fusion.10 = bf16[4,256,4096]{2,1,0:T(8,128)(2,1)} fusion(bf16[4,256,4096]{2,1,0:T(8,128)(2,1)} %get-tuple-element.38, bf16[4,256,1024]{2,1,0:T(8,128)(2,1)S(1)} %copy-done.24, bf16[4096,1024]{1,0:T(8,128)(2,1)} %param.15), kind=kOutput, calls=%fused_computation.28 | convolution fusion | flops 8686403584 | bytes 27262976 | tf_op jit(solution)/shard_map/bsd,fd->bsf/dot_general | solution.py:23
  222.4 13.9 %fusion.78 = (f32[4,256]{1,0:T(4,128)S(1)}, bf16[4,256,1024]{2,1,0:T(8,128)(2,1)S(1)}) fusion(bf16[4,256,1024]{2,1,0:T(8,128)(2,1)S(1)} %get-tuple-element.28, bf16[4,256,4096]{2,1,0:T(8,128)(2,1)} %fusion.10, bf16[1024,4096]{1,0:T(8,128)(2,1)} %param.14), kind=kOutput, calls=%fused_computation.119 | convolution fusion | flops 8595176448 | bytes 20975616 | tf_op jit(solution)/shard_map/bsf,df->bsd/dot_general | solution.py:23
  246.0 7.5 convolution_convert_fusion.3
  259.2 16.1 %fusion.153 = bf16[4,16,64,256]{3,2,1,0:T(8,128)(2,1)} fusion(bf16[4,256,16,64]{1,3,2,0:T(8,128)(2,1)} %bitcast.269, bf16[4,16,256,256]{2,3,1,0:T(8,128)(2,1)} %copy-done.1, bf16[4,16,256,256]{2,3,1,0:T(8,128)(2,1)} %convolution_convert_fusion.1), kind=kOutput, calls=%fused_computation.176 | convolution fusion | flops 575684864 | bytes 20971520 | tf_op jit(solution)/shard_map/bhqk,bkhd->bqhd/dot_general | solution.py:23
  275.3 16.9 %fusion.154 = bf16[4,16,64,256]{3,2,1,0:T(8,128)(2,1)S(1)} fusion(bf16[4,256,16,64]{1,3,2,0:T(8,128)(2,1)} %bitcast.271, bf16[4,16,256,256]{2,3,1,0:T(8,128)(2,1)} %copy-done.1, bf16[4,16,256,256]{2,3,1,0:T(8,128)(2,1)} %convolution_convert_fusion.1), kind=kOutput, calls=%fused_computation.177 | convolution fusion | flops 575684864 | bytes 20971520 | tf_op jit(solution)/shard_map/bhqk,bqhd->bkhd/dot_general | solution.py:23
  298.4 6.5 reshape.210.refs_7_
  304.9 6.6 fusion.99
  316.3 6.7 reshape.211.refs_8_
  332.7 23.4 %fusion.15 = bf16[4,256,4096]{2,1,0:T(8,128)(2,1)} fusion(bf16[4,256,4096]{2,1,0:T(8,128)(2,1)} %copy-done.51, bf16[4,256,1024]{2,1,0:T(8,128)(2,1)S(1)} %fusion.71, bf16[4096,1024]{1,0:T(8,128)(2,1)} %param.15), kind=kOutput, calls=%fused_computation.33 | convolution fusion | flops 8686403584 | bytes 27262976 | tf_op jit(solution)/shard_map/bsd,fd->bsf/dot_general | solution.py:23
  356.1 14.3 %fusion.86 = (f32[4,256]{1,0:T(4,128)S(1)}, bf16[4,256,1024]{2,1,0:T(8,128)(2,1)S(1)}) fusion(bf16[4,256,1024]{2,1,0:T(8,128)(2,1)S(1)} %copy-done.14, bf16[4,256,4096]{2,1,0:T(8,128)(2,1)} %fusion.15, bf16[1024,4096]{1,0:T(8,128)(2,1)} %param.14), kind=kOutput, calls=%fused_computation.127 | convolution fusion | flops 8595176448 | bytes 20975616 | tf_op jit(solution)/shard_map/bsf,df->bsd/dot_general | solution.py:23
  379.8 7.5 convolution_convert_fusion.2
  393.1 16.1 %fusion.151 = bf16[4,16,64,256]{3,2,1,0:T(8,128)(2,1)} fusion(bf16[4,256,16,64]{1,3,2,0:T(8,128)(2,1)} %bitcast.267, bf16[4,16,256,256]{2,3,1,0:T(8,128)(2,1)} %copy-done, bf16[4,16,256,256]{2,3,1,0:T(8,128)(2,1)} %convolution_convert_fusion), kind=kOutput, calls=%fused_computation.174 | convolution fusion | flops 575684864 | bytes 20971520 | tf_op jit(solution)/shard_map/bhqk,bkhd->bqhd/dot_general | solution.py:23
  409.2 16.9 %fusion.152 = bf16[4,16,64,256]{3,2,1,0:T(8,128)(2,1)S(1)} fusion(bf16[4,256,16,64]{1,3,2,0:T(8,128)(2,1)} %bitcast.265, bf16[4,16,256,256]{2,3,1,0:T(8,128)(2,1)} %copy-done, bf16[4,16,256,256]{2,3,1,0:T(8,128)(2,1)} %convolution_convert_fusion), kind=kOutput, calls=%fused_computation.175 | convolution fusion | flops 575684864 | bytes 20971520 | tf_op jit(solution)/shard_map/bhqk,bqhd->bkhd/dot_general | solution.py:23
  426.1 6.5 copy.111
  432.6 6.7 reshape.206.refs_1_
  439.4 6.6 fusion.115
  450.7 6.7 reshape.207.refs_2_
  462.1 6.5 reshape.208.refs_3_
  484.1 6.5 reshape.212.refs_9_
  490.6 444.9 %reduce_gradients.1 = (f32[2,1024,1024]{2,1,0:T(8,128)}, f32[2,1024,1024]{2,1,0:T(8,128)}, f32[2,1024,1024]{2,1,0:T(8,128)}, f32[2,1024,1024]{2,1,0:T(8,128)}, f...) custom-call(bf16[1024,1024]{1,0:T(8,128)(2,1)} %bitcast.260, bf16[1024,1024]{1,0:T(8,128)(2,1)} %reshape.206.refs_1_, ...), custom_call_target="tpu_custom_call" | custom-call | flops 51539607552 | bytes 134217728 | tf_op jit(solution)/shard_map/reduce_gradients/pallas_call | solution.py:426
  935.5 8.9 copy.133
  959.6 14.1 %copy.137 = f32[1024,4096]{1,0:T(8,128)} copy(f32[1024,4096]{1,0:T(8,128)} %get-tuple-element.52) | data formatting | bytes 33554432
  (176 shorter events, 188.7 us)
Async XLA Ops:
  0.6 6.2 copy-start.45
  13.6 38.0 %copy-start.4 = (bf16[4,256,1024]{1,2,0:T(8,128)(2,1)}, bf16[4,256,1024]{1,2,0:T(8,128)(2,1)S(1)}, u32[]{:S(2)}) copy-start(bf16[4,256,1024]{1,2,0:T(8,128)(2,1)S(1)} %copy.57) | copy-start | bytes 6291460
  51.5 4.3 copy-start
  51.5 6.6 copy-start.41
  55.8 5.2 copy-start.22
  61.0 32.0 %copy-start.13 = (bf16[4,256,1024]{2,1,0:T(8,128)(2,1)}, bf16[4,256,1024]{2,1,0:T(8,128)(2,1)S(1)}, u32[]{:S(2)}) copy-start(bf16[4,256,1024]{2,1,0:T(8,128)(2,1)S(1)} %get-tuple-element.22) | copy-start | bytes 6291460
  93.0 17.9 %copy-start.51 = (bf16[4,256,4096]{2,1,0:T(8,128)(2,1)}, bf16[4,256,4096]{2,1,0:T(8,128)(2,1)S(1)}, u32[]{:S(2)}) copy-start(bf16[4,256,4096]{2,1,0:T(8,128)(2,1)S(1)} %get-tuple-element.36) | copy-start | bytes 25165828
  112.9 18.0 %copy-start.28 = (bf16[4,256,1024]{2,1,0:T(8,128)(2,1)}, bf16[4,256,1024]{2,1,0:T(8,128)(2,1)S(1)}, u32[]{:S(2)}) copy-start(bf16[4,256,1024]{2,1,0:T(8,128)(2,1)S(1)} %fusion.88) | copy-start | bytes 6291460
  139.0 18.5 %copy-start.6 = (bf16[4,256,1024]{1,2,0:T(8,128)(2,1)}, bf16[4,256,1024]{1,2,0:T(8,128)(2,1)S(1)}, u32[]{:S(2)}) copy-start(bf16[4,256,1024]{1,2,0:T(8,128)(2,1)S(1)} %copy.60) | copy-start | bytes 6291460
  157.4 4.3 copy-start.1
  157.5 6.6 copy-start.42
  161.7 5.2 copy-start.23
  181.4 18.2 %copy-start.24 = (bf16[4,256,1024]{2,1,0:T(8,128)(2,1)S(1)}, bf16[4,256,1024]{2,1,0:T(8,128)(2,1)}, u32[]{:S(2)}) copy-start(bf16[4,256,1024]{2,1,0:T(8,128)(2,1)} %param.9) | copy-start | bytes 6291460
  246.0 7.5 copy-start.7
  323.0 5.3 copy-start.50
  332.7 37.8 %copy-start.18 = (bf16[4,256,1024]{2,1,0:T(8,128)(2,1)}, bf16[4,256,1024]{2,1,0:T(8,128)(2,1)S(1)}, u32[]{:S(2)}) copy-start(bf16[4,256,1024]{2,1,0:T(8,128)(2,1)S(1)} %fusion.71) | copy-start | bytes 6291460
  332.7 23.4 %copy-start.14 = (bf16[4,256,1024]{2,1,0:T(8,128)(2,1)S(1)}, bf16[4,256,1024]{2,1,0:T(8,128)(2,1)}, u32[]{:S(2)}) copy-start(bf16[4,256,1024]{2,1,0:T(8,128)(2,1)} %copy-done.13) | copy-start | bytes 6291460
  356.1 14.3 %copy-start.38 = (f32[4,256]{1,0:T(4,128)S(1)}, f32[4,256]{1,0:T(4,128)}, u32[]{:S(2)}) copy-start(f32[4,256]{1,0:T(4,128)} %copy-done.37) | copy-start | bytes 12292
  356.1 14.4 %copy-start.32 = (f32[4,256]{1,0:T(4,128)S(1)}, f32[4,256]{1,0:T(4,128)}, u32[]{:S(2)}) copy-start(f32[4,256]{1,0:T(4,128)} %copy-done.31) | copy-start | bytes 12292
  379.8 7.5 copy-start.5
  426.1 19.9 %copy-start.25 = (bf16[4,16,64,256]{3,2,1,0:T(8,128)(2,1)}, bf16[4,16,64,256]{3,2,1,0:T(8,128)(2,1)S(1)}, u32[]{:S(2)}) copy-start(bf16[4,16,64,256]{3,2,1,0:T(8,128)(2,1)S(1)} %fusion.152) | copy-start | bytes 6291460
  450.7 6.7 copy-start.10
  468.7 5.3 copy-start.49
  935.5 8.9 copy-start.21
  935.5 13.1 %slice-start.6 = ((s8[8388608]{0:T(1024)(128)(4,1)}), s8[4194304]{0:T(1024)(128)(4,1)S(1)}, s32[]{:S(2)}) async-start(s8[8388608]{0:T(1024)(128)(4,1)} %bitcast.245), calls=%async_computation.6 | async-start | bytes 8388608
  944.4 5.2 slice-start.7
  944.4 9.5 slice-start.4
  949.6 5.7 slice-start.5
  955.3 18.4 %slice-start = ((s8[16777216]{0:T(1024)(128)(4,1)}), s8[4194304]{0:T(1024)(128)(4,1)S(1)}, s32[]{:S(2)}) async-start(s8[16777216]{0:T(1024)(128)(4,1)} %bitcast.234), calls=%async_computation | async-start | bytes 8388608
  955.3 18.4 %slice-start.1 = ((s8[16777216]{0:T(1024)(128)(4,1)}), s8[4194304]{0:T(1024)(128)(4,1)S(1)}, s32[]{:S(2)}) async-start(s8[16777216]{0:T(1024)(128)(4,1)} %bitcast.234), calls=%async_computation.1 | async-start | bytes 8388608
  959.6 14.2 %slice-start.2 = ((s8[16777216]{0:T(1024)(128)(4,1)}), s8[4194304]{0:T(1024)(128)(4,1)S(1)}, s32[]{:S(2)}) async-start(s8[16777216]{0:T(1024)(128)(4,1)} %bitcast.234), calls=%async_computation.2 | async-start | bytes 8388608
  959.6 15.5 %slice-start.3 = ((s8[16777216]{0:T(1024)(128)(4,1)}), s8[4194304]{0:T(1024)(128)(4,1)S(1)}, s32[]{:S(2)}) async-start(s8[16777216]{0:T(1024)(128)(4,1)} %bitcast.234), calls=%async_computation.3 | async-start | bytes 8388608
  (28 other events, 76.0 us)

commit v2 on v1

--- a/solution.py
+++ b/solution.py
@@ -9,68 +9,259 @@
 
 EPS = 1e-6
 HEAD_DIM = 64
+PAIR = 2 * HEAD_DIM
+FF_BLOCK = 512
+OUT_BLOCK = 256
+GELU_A = (2.0 / 3.141592653589793) ** 0.5
+GELU_B = 0.044715
+MIB = 1024 * 1024
+
+
+def dot(lhs, rhs, lhs_dim, rhs_dim):
+    return lax.dot_general(lhs, rhs, (((lhs_dim,), (rhs_dim,)), ((), ())), preferred_element_type=jnp.float32)
 
 
 def rms_norm(x_f32):
     return x_f32 * lax.rsqrt(jnp.mean(x_f32 * x_f32, axis=-1, keepdims=True) + EPS)
 
 
-def gelu_tanh(pre_f32):
-    return jax.nn.gelu(pre_f32, approximate=True)
-
-
-def product(subscripts, lhs, rhs):
-    return jnp.einsum(subscripts, lhs, rhs, preferred_element_type=jnp.float32)
-
-
-def layer_forward(x_act, w_query, w_key, w_value, w_proj, w_up, w_down, heads):
-    batch, seq_len, width = x_act.shape
-    head_dim = width // heads
-    x_f32 = x_act.astype(jnp.float32)
-    normed = rms_norm(x_f32).astype(jnp.bfloat16)
-    query = product("bsd,de->bse", normed, w_query).astype(jnp.bfloat16).reshape(batch, seq_len, heads, head_dim)
-    key_act = product("bsd,de->bse", normed, w_key).astype(jnp.bfloat16).reshape(batch, seq_len, heads, head_dim)
-    value = product("bsd,de->bse", normed, w_value).astype(jnp.bfloat16).reshape(batch, seq_len, heads, head_dim)
-    scores = product("bqhd,bkhd->bhqk", query, key_act) * head_dim ** -0.5
-    probs = jax.nn.softmax(scores, axis=-1).astype(jnp.bfloat16)
-    mixed = product("bhqk,bkhd->bqhd", probs, value).astype(jnp.bfloat16).reshape(batch, seq_len, width)
-    attn_out = product("bsd,de->bse", mixed, w_proj).astype(jnp.bfloat16)
-    hidden = (x_f32 + attn_out.astype(jnp.float32)).astype(jnp.bfloat16)
-    normed2 = rms_norm(hidden.astype(jnp.float32)).astype(jnp.bfloat16)
-    pre_act = product("bsd,df->bsf", normed2, w_up).astype(jnp.bfloat16)
-    activated = gelu_tanh(pre_act.astype(jnp.float32)).astype(jnp.bfloat16)
-    mlp_out = product("bsf,fd->bsd", activated, w_down).astype(jnp.bfloat16)
-    x_next = (hidden.astype(jnp.float32) + mlp_out.astype(jnp.float32)).astype(jnp.bfloat16)
-    kept = (x_act, normed, query, key_act, value, probs, mixed, hidden, normed2, pre_act, activated)
-    return x_next, kept
-
-
-def layer_backward(d_next, kept, w_query, w_key, w_value, w_proj, w_up, w_down):
-    x_act, normed, query, key_act, value, probs, mixed, hidden, normed2, pre_act, activated = kept
-    batch, seq_len, heads, head_dim = query.shape
-    width = heads * head_dim
-    d_activated = product("bsd,fd->bsf", d_next, w_down).astype(jnp.bfloat16)
-    gelu_pull = jax.vjp(gelu_tanh, pre_act.astype(jnp.float32))[1]
-    d_pre = gelu_pull(d_activated.astype(jnp.float32))[0].astype(jnp.bfloat16)
-    d_normed2 = product("bsf,df->bsd", d_pre, w_up).astype(jnp.bfloat16)
-    hidden_pull = jax.vjp(rms_norm, hidden.astype(jnp.float32))[1]
-    d_hidden = (d_next.astype(jnp.float32) + hidden_pull(d_normed2.astype(jnp.float32))[0]).astype(jnp.bfloat16)
-    d_mixed = product("bse,de->bsd", d_hidden, w_proj).astype(jnp.bfloat16).reshape(batch, seq_len, heads, head_dim)
-    d_probs = product("bqhd,bkhd->bhqk", d_mixed, value).astype(jnp.bfloat16).astype(jnp.float32)
-    d_value = product("bhqk,bqhd->bkhd", probs, d_mixed).astype(jnp.bfloat16).reshape(batch, seq_len, width)
-    probs_f32 = probs.astype(jnp.float32)
-    row_dot = jnp.sum(d_probs * probs_f32, axis=-1, keepdims=True)
-    d_scores = (probs_f32 * (d_probs - row_dot) * head_dim ** -0.5).astype(jnp.bfloat16)
-    d_query = product("bhqk,bkhd->bqhd", d_scores, key_act).astype(jnp.bfloat16).reshape(batch, seq_len, width)
-    d_key = product("bhqk,bqhd->bkhd", d_scores, query).astype(jnp.bfloat16).reshape(batch, seq_len, width)
-    d_normed = (product("bse,de->bsd", d_query, w_query) + product("bse,de->bsd", d_key, w_key)
-                + product("bse,de->bsd", d_value, w_value)).astype(jnp.bfloat16)
-    input_pull = jax.vjp(rms_norm, x_act.astype(jnp.float32))[1]
-    d_input = (d_hidden.astype(jnp.float32) + input_pull(d_normed.astype(jnp.float32))[0]).astype(jnp.bfloat16)
-    attn = (normed, d_query, d_key, d_value, mixed, d_hidden)
-    mlp = (normed2, d_pre, activated, d_next)
-    flat = lambda arr: arr.reshape(batch * seq_len, -1)
-    return d_input, tuple(map(flat, attn)), tuple(map(flat, mlp))
+def rms_backward(x_f32, d_out):
+    scale = lax.rsqrt(jnp.mean(x_f32 * x_f32, axis=-1, keepdims=True) + EPS)
+    inner = jnp.mean(x_f32 * d_out, axis=-1, keepdims=True)
+    return scale * d_out - x_f32 * (scale * scale * scale * inner)
+
+
+def gelu_parts(pre):
+    square = pre * pre
+    tanh = jnp.tanh(GELU_A * (pre + GELU_B * pre * square))
+    half = 0.5 * (1.0 + tanh)
+    slope = half + 0.5 * pre * (1.0 - tanh * tanh) * (GELU_A + (3.0 * GELU_A * GELU_B) * square)
+    return pre * half, slope
+
+
+def call(kernel, grid, in_specs, outs, scratch=(), flops=0, moved=0, name=None):
+    return pl.pallas_call(
+        kernel,
+        grid=grid,
+        in_specs=in_specs,
+        out_specs=[spec for _, spec in outs],
+        out_shape=[shape for shape, _ in outs],
+        scratch_shapes=list(scratch),
+        compiler_params=pltpu.CompilerParams(vmem_limit_bytes=60 * MIB, dimension_semantics=("arbitrary",) * len(grid)),
+        cost_estimate=pl.CostEstimate(flops=flops, bytes_accessed=moved, transcendentals=0),
+        name=name,
+    )
+
+
+def whole(shape):
+    return pl.BlockSpec(shape, lambda *_: (0,) * len(shape), pipeline_mode=pl.Buffered(1))
+
+
+def bf16(*shape):
+    return jax.ShapeDtypeStruct(shape, jnp.bfloat16)
+
+
+def project_qkv(x_act, w_query, w_key, w_value, layer):
+    tokens, width = x_act.shape
+
+    def kernel(x_ref, wq_ref, wk_ref, wv_ref, u_ref, q_ref, k_ref, v_ref):
+        @pl.when(pl.program_id(0) == 0)
+        def _():
+            u_ref[...] = rms_norm(x_ref[...].astype(jnp.float32)).astype(jnp.bfloat16)
+
+        for w_ref, o_ref in ((wq_ref, q_ref), (wk_ref, k_ref), (wv_ref, v_ref)):
+            o_ref[...] = dot(u_ref[...], w_ref[...], 1, 0).astype(jnp.bfloat16)
+
+    weight = pl.BlockSpec((None, width, OUT_BLOCK), lambda i: (layer, 0, i))
+    block = pl.BlockSpec((tokens, OUT_BLOCK), lambda i: (0, i))
+    return call(
+        kernel, (width // OUT_BLOCK,), [whole((tokens, width)), weight, weight, weight],
+        [(bf16(tokens, width), whole((tokens, width)))] + [(bf16(tokens, width), block)] * 3,
+        flops=6 * tokens * width * width, moved=14 * tokens * width, name=f"qkv_{layer}")(x_act, w_query, w_key, w_value)
+
+
+def attend(x_act, query, key_act, value, w_proj, layer, seq):
+    tokens, width = x_act.shape
+    heads = width // HEAD_DIM
+
+    def kernel(x_ref, q_ref, k_ref, v_ref, wo_ref, p_ref, mix_ref, h_ref, n_ref):
+        low = lax.broadcasted_iota(jnp.int32, (seq, PAIR), 1) < HEAD_DIM
+
+        def pair(j, carry):
+            lanes = pl.ds(pl.multiple_of(PAIR * j, PAIR), PAIR)
+            q_pair, k_pair, v_pair = q_ref[:, lanes], k_ref[:, lanes], v_ref[:, lanes]
+            total = None
+            for side in range(2):
+                mask = low if side == 0 else jnp.logical_not(low)
+                scores = dot(jnp.where(mask, q_pair, 0), k_pair, 1, 1) * HEAD_DIM ** -0.5
+                top = jnp.max(scores, axis=-1, keepdims=True)
+                raised = jnp.exp(scores - top)
+                inverse = 1.0 / jnp.sum(raised, axis=-1, keepdims=True)
+                probs = (raised * inverse).astype(jnp.bfloat16)
+                p_ref[2 * j + side] = probs
+                part = dot(probs, jnp.where(mask, v_pair, 0), 1, 0)
+                total = part if total is None else total + part
+            mix_ref[:, lanes] = total.astype(jnp.bfloat16)
+            return carry
+
+        lax.fori_loop(0, heads // 2, pair, 0)
+        attn = dot(mix_ref[...], wo_ref[...], 1, 0).astype(jnp.bfloat16)
+        hidden = (x_ref[...].astype(jnp.float32) + attn.astype(jnp.float32)).astype(jnp.bfloat16)
+        h_ref[...] = hidden
+        n_ref[...] = rms_norm(hidden.astype(jnp.float32)).astype(jnp.bfloat16)
+
+    row = pl.BlockSpec((seq, width), lambda i: (i, 0))
+    weight = pl.BlockSpec((None, width, width), lambda i: (layer, 0, 0), pipeline_mode=pl.Buffered(1))
+    probs = pl.BlockSpec((None, heads, seq, seq), lambda i: (i, 0, 0, 0))
+    act = (bf16(tokens, width), row)
+    return call(
+        kernel, (tokens // seq,), [row, row, row, row, weight], [(bf16(tokens // seq, heads, seq, seq), probs), act, act, act],
+        flops=2 * tokens * width * (width + 2 * seq), moved=20 * tokens * width, name=f"attend_{layer}",
+    )(x_act, query, key_act, value, w_proj)
+
+
+def mlp_forward(hidden, normed2, w_up, w_down):
+    tokens, width = hidden.shape
+    ff = w_up.shape[1]
+    steps = ff // FF_BLOCK
+
+    def kernel(h_ref, n_ref, w1_ref, w2_ref, pre_ref, act_ref, x_ref, acc_ref):
+        i = pl.program_id(0)
+        pre = dot(n_ref[...], w1_ref[...], 1, 0).astype(jnp.bfloat16)
+        pre_ref[...] = pre
+        act = gelu_parts(pre.astype(jnp.float32))[0].astype(jnp.bfloat16)
+        act_ref[...] = act
+        part = dot(act, w2_ref[...], 1, 0)
+
+        @pl.when(i == 0)
+        def _():
+            acc_ref[...] = part
+
+        @pl.when(i > 0)
+        def _():
+            acc_ref[...] += part
+
+        @pl.when(i == steps - 1)
+        def _():
+            out = acc_ref[...].astype(jnp.bfloat16).astype(jnp.float32)
+            x_ref[...] = (h_ref[...].astype(jnp.float32) + out).astype(jnp.bfloat16)
+
+    full = whole((tokens, width))
+    up = pl.BlockSpec((width, FF_BLOCK), lambda i: (0, i))
+    down = pl.BlockSpec((FF_BLOCK, width), lambda i: (i, 0))
+    wide = pl.BlockSpec((tokens, FF_BLOCK), lambda i: (0, i))
+    return call(
+        kernel, (steps,), [full, full, up, down],
+        [(bf16(tokens, ff), wide), (bf16(tokens, ff), wide), (bf16(tokens, width), full)],
+        [pltpu.VMEM((tokens, width), jnp.float32)], flops=4 * tokens * width * ff, moved=4 * tokens * ff + 4 * width * ff,
+        name="mlp_forward")(hidden, normed2, w_up, w_down)
+
+
+def mlp_backward(d_next, hidden, feed, w_up, w_down, replay, name):
+    tokens, width = hidden.shape
+    ff = w_up.shape[1]
+    steps = ff // FF_BLOCK
+
+    def kernel(d_ref, h_ref, feed_ref, w1_ref, w2_ref, *refs):
+        outs, acc_ref = refs[:-1], refs[-1]
+        i = pl.program_id(0)
+        if replay:
+            pre = dot(feed_ref[...], w1_ref[...], 1, 0).astype(jnp.bfloat16)
+        else:
+            pre = feed_ref[...]
+        act, slope = gelu_parts(pre.astype(jnp.float32))
+        if replay:
+            outs[2][...] = act.astype(jnp.bfloat16)
+        d_act = dot(d_ref[...], w2_ref[...], 1, 1).astype(jnp.bfloat16)
+        d_pre = (d_act.astype(jnp.float32) * slope).astype(jnp.bfloat16)
+        outs[0][...] = d_pre
+        part = dot(d_pre, w1_ref[...], 1, 1)
+
+        @pl.when(i == 0)
+        def _():
+            acc_ref[...] = part
+
+        @pl.when(i > 0)
+        def _():
+            acc_ref[...] += part
+
+        @pl.when(i == steps - 1)
+        def _():
+            d_normed = acc_ref[...].astype(jnp.bfloat16).astype(jnp.float32)
+            back = rms_backward(h_ref[...].astype(jnp.float32), d_normed)
+            outs[1][...] = (d_ref[...].astype(jnp.float32) + back).astype(jnp.bfloat16)
+
+    full = whole((tokens, width))
+    up = pl.BlockSpec((width, FF_BLOCK), lambda i: (0, i))
+    down = pl.BlockSpec((FF_BLOCK, width), lambda i: (i, 0))
+    wide = pl.BlockSpec((tokens, FF_BLOCK), lambda i: (0, i))
+    outs = [(bf16(tokens, ff), wide), (bf16(tokens, width), full)] + ([(bf16(tokens, ff), wide)] if replay else [])
+    return call(
+        kernel, (steps,), [full, full, full if replay else wide, up, down], outs,
+        [pltpu.VMEM((tokens, width), jnp.float32)], flops=(6 if replay else 4) * tokens * width * ff,
+        moved=4 * tokens * ff + 4 * width * ff, name=name)(d_next, hidden, feed, w_up, w_down)
+
+
+def attend_backward(d_hidden, query, key_act, value, probs, w_proj, layer, seq):
+    tokens, width = d_hidden.shape
+    heads = width // HEAD_DIM
+
+    def kernel(d_ref, q_ref, k_ref, v_ref, p_ref, wo_ref, dq_ref, dk_ref, dv_ref, mix_ref):
+        mix_ref[...] = dot(d_ref[...], wo_ref[...], 1, 1).astype(jnp.bfloat16)
+        low = lax.broadcasted_iota(jnp.int32, (seq, PAIR), 1) < HEAD_DIM
+
+        def pair(j, carry):
+            lanes = pl.ds(pl.multiple_of(PAIR * j, PAIR), PAIR)
+            q_pair, k_pair, v_pair, d_pair = q_ref[:, lanes], k_ref[:, lanes], v_ref[:, lanes], mix_ref[:, lanes]
+            sums = [None] * 3
+            for side in range(2):
+                mask = low if side == 0 else jnp.logical_not(low)
+                d_side = jnp.where(mask, d_pair, 0)
+                probs_16 = p_ref[2 * j + side]
+                probs_32 = probs_16.astype(jnp.float32)
+                d_probs = dot(d_side, v_pair, 1, 1).astype(jnp.bfloat16).astype(jnp.float32)
+                row_dot = jnp.sum(d_probs * probs_32, axis=-1, keepdims=True)
+                d_scores = (probs_32 * (d_probs - row_dot) * HEAD_DIM ** -0.5).astype(jnp.bfloat16)
+                parts = (dot(d_scores, jnp.where(mask, k_pair, 0), 1, 0),
+                         dot(d_scores, jnp.where(mask, q_pair, 0), 0, 0),
+                         dot(probs_16, d_side, 0, 0))
+                sums = [part if total is None else total + part for total, part in zip(sums, parts)]
+            for ref, total in zip((dq_ref, dk_ref, dv_ref), sums):
+                ref[:, lanes] = total.astype(jnp.bfloat16)
+            return carry
+
+        lax.fori_loop(0, heads // 2, pair, 0)
+
+    row = pl.BlockSpec((seq, width), lambda i: (i, 0))
+    weight = pl.BlockSpec((None, width, width), lambda i: (layer, 0, 0), pipeline_mode=pl.Buffered(1))
+    block = pl.BlockSpec((None, heads, seq, seq), lambda i: (i, 0, 0, 0))
+    act = (bf16(tokens, width), row)
+    return call(
+        kernel, (tokens // seq,), [row, row, row, row, block, weight], [act, act, act],
+        [pltpu.VMEM((seq, width), jnp.bfloat16)], flops=2 * tokens * width * (width + 4 * seq), moved=24 * tokens * width,
+        name=f"attend_backward_{layer}")(d_hidden, query, key_act, value, probs, w_proj)
+
+
+def project_backward(x_act, d_hidden, d_query, d_key, d_value, w_query, w_key, w_value, layer):
+    tokens, width = x_act.shape
+    steps = width // OUT_BLOCK
+
+    def kernel(x_ref, d_ref, dq_ref, dk_ref, dv_ref, wq_ref, wk_ref, wv_ref, o_ref, sum_ref):
+        i = pl.program_id(0)
+        total = dot(dq_ref[...], wq_ref[...], 1, 1) + dot(dk_ref[...], wk_ref[...], 1, 1) + dot(dv_ref[...], wv_ref[...], 1, 1)
+        sum_ref[:, pl.ds(pl.multiple_of(OUT_BLOCK * i, OUT_BLOCK), OUT_BLOCK)] = total.astype(jnp.bfloat16)
+
+        @pl.when(i == steps - 1)
+        def _():
+            back = rms_backward(x_ref[...].astype(jnp.float32), sum_ref[...].astype(jnp.float32))
+            o_ref[...] = (d_ref[...].astype(jnp.float32) + back).astype(jnp.bfloat16)
+
+    full = whole((tokens, width))
+    weight = pl.BlockSpec((None, OUT_BLOCK, width), lambda i: (layer, i, 0))
+    return call(
+        kernel, (steps,), [full] * 5 + [weight] * 3, [(bf16(tokens, width), full)],
+        [pltpu.VMEM((tokens, width), jnp.bfloat16)], flops=6 * tokens * width * width, moved=18 * tokens * width,
+        name=f"project_backward_{layer}")(x_act, d_hidden, d_query, d_key, d_value, w_query, w_key, w_value)[0]
 
 
 MESH = pl.DeviceIdType.MESH
@@ -435,6 +626,7 @@
         name="reduce_gradients",
     )(*operands)
 
+
 def gradient_groups(width, ff):
     groups = []
 
@@ -461,25 +653,39 @@
     return groups, sum(group["count"] for group in groups)
 
 
+def local_operands(x_init, cot_out, w_query, w_key, w_value, w_proj, w_up, w_down):
+    batch, seq, width = x_init.shape
+    x_in = [x_init.reshape(batch * seq, width), None]
+    d_act = cot_out.reshape(batch * seq, width)
+    kept = []
+    for layer in (0, 1):
+        normed, query, key_act, value = project_qkv(x_in[layer], w_query, w_key, w_value, layer)
+        probs, mixed, hidden, normed2 = attend(x_in[layer], query, key_act, value, w_proj, layer, seq)
+        kept.append((normed, query, key_act, value, probs, mixed, hidden, normed2))
+        if layer == 0:
+            pre_act, act_0, x_in[1] = mlp_forward(hidden, normed2, w_up, w_down)
+    attn, mlp = [None, None], [None, None]
+    for layer in (1, 0):
+        normed, query, key_act, value, probs, mixed, hidden, normed2 = kept[layer]
+        if layer == 1:
+            d_pre, d_hidden, act = mlp_backward(d_act, hidden, normed2, w_up, w_down, True, "mlp_both")
+        else:
+            d_pre, d_hidden = mlp_backward(d_act, hidden, pre_act, w_up, w_down, False, "mlp_backward")
+            act = act_0
+        mlp[layer] = (normed2, d_pre, act, d_act)
+        d_query, d_key, d_value = attend_backward(d_hidden, query, key_act, value, probs, w_proj, layer, seq)
+        d_act = project_backward(x_in[layer], d_hidden, d_query, d_key, d_value, w_query, w_key, w_value, layer)
+        attn[layer] = (normed, d_query, d_key, d_value, mixed, d_hidden)
+    return [*attn[0], *attn[1], *mlp[0], *mlp[1]], d_act.reshape(batch, seq, width)
+
+
 def solution(mesh):
     def local_step(x_init, cot_out, w_query, w_key, w_value, w_proj, w_up, w_down):
-        batch, seq_len, width = x_init.shape
-        heads = width // HEAD_DIM
-        x_act = x_init
-        kept_all = []
-        for layer in range(2):
-            x_act, kept = layer_forward(x_act, w_query[layer], w_key[layer], w_value[layer], w_proj[layer], w_up, w_down, heads)
-            kept_all.append(kept)
-        d_act = cot_out
-        attn, mlp = [None] * 2, [None] * 2
-        for layer in (1, 0):
-            d_act, attn[layer], mlp[layer] = layer_backward(
-                d_act, kept_all[layer], w_query[layer], w_key[layer], w_value[layer], w_proj[layer], w_up, w_down)
-        operands = [*attn[0], *attn[1], *mlp[0], *mlp[1]]
-        groups, chunks = gradient_groups(width, w_up.shape[1])
+        operands, d_init = local_operands(x_init, cot_out, w_query, w_key, w_value, w_proj, w_up, w_down)
+        groups, chunks = gradient_groups(x_init.shape[2], w_up.shape[1])
         shapes = [w_query.shape, w_key.shape, w_value.shape, w_proj.shape, w_up.shape, w_down.shape]
-        grads = reduce_gradients(operands, groups, chunks, shapes, batch * seq_len)
-        return (*grads, d_act)
+        grads = reduce_gradients(operands, groups, chunks, shapes, operands[0].shape[0])
+        return (*grads, d_init)
 
     data_spec = P("data")
     full_spec = P()

time: 986 us -> 761 us (0.77)
  matrix products: 316 us -> 0 us
  Pallas kernels: 445 us -> 714 us
  local copies, waits for them, and re-layouts: 191 us -> 45.7 us
  other arithmetic: 28.2 us -> 0.01 us
    dot_general x33 -> x0, matrix products: 294 us -> none  [product(): return jnp.einsum(subscripts, lhs, rhs, preferred_element_type=jnp.float32)]
    pallas_call x0 -> x11, Pallas kernels: none -> 269 us  [the longest x2 74.1 us: mlp_backward(): call(kernel, (steps,), [full, full, full if replay else wide, up, down],...]
    another operation x16 -> x0, local copies, waits for them, and re-layouts: 97.1 us -> none  [layer_backward(): flat = lambda arr: arr.reshape(batch * seq_len, -1)]
    convert_element_type x8 -> x0, local copies, waits for them, and re-layouts: 27.8 us -> none  [the longest x2 7.93 us: layer_forward(): product('bsd,de->bse', normed, w_key).astype(jnp.bfloat16)]
    convert_element_type x10 -> x0, other arithmetic: 25.9 us -> none  [the longest x2 13.7 us: layer_forward(): probs = jax.nn.softmax(scores, axis=-1).astype(jnp.bfloat16)]
    sub x2 -> x0, matrix products: 22.2 us -> none  [layer_forward(): probs = jax.nn.softmax(scores, axis=-1).astype(jnp.bfloat16)]
    unnamed x126 -> x24, local copies, waits for them, and re-layouts: 66 us -> 45.7 us
where the time goes in v2:
time: 761 us; the launch traced here: 760 us
  Pallas kernels  714 us (94%)
  local copies, waits for them, and re-layouts  45.7 us (6%)
    pallas_call x1, Pallas kernels, reduce_gradients(): pl.pallas_call(functools.partial(reduce_kernel, groups, chunks, len(opera...  445 us
    pallas_call x2, Pallas kernels, mlp_backward(): call(kernel, (steps,), [full, full, full if replay else wide, up, down],...  74.1 us
    pallas_call x2, Pallas kernels, attend_backward(): call(kernel, (tokens // seq,), [row, row, row, row, block, weight], [act,...  61.8 us
    pallas_call x2, Pallas kernels, attend(): call(kernel, (tokens // seq,), [row, row, row, row, weight], [(bf16(token...  49.6 us
    unnamed x24, local copies, waits for them, and re-layouts  45.7 us
    pallas_call x1, Pallas kernels, mlp_forward(): call(kernel, (steps,), [full, full, up, down], [(bf16(tokens, ff), wide),...  30.5 us
    pallas_call x2, Pallas kernels, project_backward(): call(kernel, (steps,), [full] * 5 + [weight] * 3, [(bf16(tokens, width),...  30.3 us
    pallas_call x2, Pallas kernels, project_qkv(): call(kernel, (width // OUT_BLOCK,), [whole((tokens, width)), weight, weig...  22.7 us

profile of v2, /device:TPU:0, one launch (start us, length us, event | category | flops | bytes accessed | tf_op | source)
XLA Modules:
  0.0 760.3 jit_solution(8514456199517153438)
XLA Ops:
  0.6 11.4 %qkv_0.1 = (bf16[1024,1024]{1,0:T(8,128)(2,1)}, bf16[1024,1024]{1,0:T(8,128)(2,1)}, bf16[1024,1024]{1,0:T(8,128)(2,1)}, bf16[1024,1024]{1,0:T(8,128)(2,1)}) custom-call(bf16[1024,1024]{1,0:T(8,128)(2,1)} %bitcast.9, bf16[2,1024,1024]{2,1,0:T(8,128)(2,1)} %wq_ref.7, bf16[2,1024,1024]{2,1,0:T(8,128)(2,1)} %wk_ref.7, bf16[2,1024,1024]{2,1,0:T(8,128)(2,1)} %wv_ref.7), custom_call_target="tpu_custom_call" | custom-call | flops 6442450944 | bytes 14680064 | tf_op jit(solution)/shard_map/qkv_0/pallas_call | solution.py:77
  12.0 24.8 %attend_0.1 = (bf16[4,16,256,256]{3,2,1,0:T(8,128)(2,1)}, bf16[1024,1024]{1,0:T(8,128)(2,1)}, bf16[1024,1024]{1,0:T(8,128)(2,1)}, bf16[1024,1024]{1,0:T(8,128)(2,1)}) custom-call(bf16[1024,1024]{1,0:T(8,128)(2,1)} %bitcast.10, bf16[1024,1024]{1,0:T(8,128)(2,1)} %get-tuple-element.44.q_ref, bf16[1024,1024]{1,0:T(8,128)(2,1)} %get-tuple-element.45.k_ref, ...), custom_call_target="tpu_custom_call" | custom-call | flops 3221225472 | bytes 20971520 | tf_op jit(solution)/shard_map/attend_0/pallas_call | solution.py:117
  36.8 30.5 %mlp_forward.1 = (bf16[1024,4096]{1,0:T(8,128)(2,1)}, bf16[1024,4096]{1,0:T(8,128)(2,1)}, bf16[1024,1024]{1,0:T(8,128)(2,1)}) custom-call(bf16[1024,1024]{1,0:T(8,128)(2,1)} %get-tuple-element.47.h_ref, bf16[1024,1024]{1,0:T(8,128)(2,1)} %get-tuple-element.48.n_ref.refs_12_, bf16[1024,4096]{1,0:T(8,128)(2,1)} %w1_ref.5, bf16[4096,1024]{1,0:T(8,128)(2,1)} %w2_ref.5), custom_call_target="tpu_custom_call" | custom-call | flops 17179869184 | bytes 33554432 | tf_op jit(solution)/shard_map/mlp_forward/pallas_call | solution.py:153
  67.3 11.4 %qkv_1.1 = (bf16[1024,1024]{1,0:T(8,128)(2,1)}, bf16[1024,1024]{1,0:T(8,128)(2,1)}, bf16[1024,1024]{1,0:T(8,128)(2,1)}, bf16[1024,1024]{1,0:T(8,128)(2,1)}) custom-call(bf16[1024,1024]{1,0:T(8,128)(2,1)} %get-tuple-element.49.x_ref, bf16[2,1024,1024]{2,1,0:T(8,128)(2,1)} %wq_ref.7, bf16[2,1024,1024]{2,1,0:T(8,128)(2,1)} %wk_ref.7, bf16[2,1024,1024]{2,1,0:T(8,128)(2,1)} %wv_ref.7), custom_call_target="tpu_custom_call" | custom-call | flops 6442450944 | bytes 14680064 | tf_op jit(solution)/shard_map/qkv_1/pallas_call | solution.py:77
  78.6 24.8 %attend_1.1 = (bf16[4,16,256,256]{3,2,1,0:T(8,128)(2,1)}, bf16[1024,1024]{1,0:T(8,128)(2,1)}, bf16[1024,1024]{1,0:T(8,128)(2,1)}, bf16[1024,1024]{1,0:T(8,128)(2,1)}) custom-call(bf16[1024,1024]{1,0:T(8,128)(2,1)} %get-tuple-element.49.x_ref, bf16[1024,1024]{1,0:T(8,128)(2,1)} %get-tuple-element.50.q_ref, bf16[1024,1024]{1,0:T(8,128)(2,1)} %get-tuple-element.51.k_ref, ...), custom_call_target="tpu_custom_call" | custom-call | flops 3221225472 | bytes 20971520 | tf_op jit(solution)/shard_map/attend_1/pallas_call | solution.py:117
  103.4 38.7 %mlp_both.1 = (bf16[1024,4096]{1,0:T(8,128)(2,1)}, bf16[1024,1024]{1,0:T(8,128)(2,1)}, bf16[1024,4096]{1,0:T(8,128)(2,1)}) custom-call(bf16[1024,1024]{1,0:T(8,128)(2,1)} %bitcast.13, bf16[1024,1024]{1,0:T(8,128)(2,1)} %get-tuple-element.53.h_ref, bf16[1024,1024]{1,0:T(8,128)(2,1)} %get-tuple-element.54.feed_ref.refs_16_, bf16[1024,4096]{1,0:T(8,128)(2,1)} %w1_ref.5, ...), custom_call_target="tpu_custom_call" | custom-call | flops 25769803776 | bytes 33554432 | tf_op jit(solution)/shard_map/mlp_both/pallas_call | solution.py:199
  142.2 30.9 %attend_backward_1.1 = (bf16[1024,1024]{1,0:T(8,128)(2,1)}, bf16[1024,1024]{1,0:T(8,128)(2,1)}, bf16[1024,1024]{1,0:T(8,128)(2,1)}) custom-call(bf16[1024,1024]{1,0:T(8,128)(2,1)} %get-tuple-element.55.d_ref.refs_11_, bf16[1024,1024]{1,0:T(8,128)(2,1)} %get-tuple-element.50.q_ref, bf16[1024,1024]{1,0:T(8,128)(2,1)} %get-tuple-element.51.k_ref, ...), custom_call_target="tpu_custom_call" | custom-call | flops 4294967296 | bytes 25165824 | tf_op jit(solution)/shard_map/attend_backward_1/pallas_call | solution.py:239
  173.0 15.2 %project_backward_1.1.d_ref.refs_15_ = bf16[1024,1024]{1,0:T(8,128)(2,1)} custom-call(bf16[1024,1024]{1,0:T(8,128)(2,1)} %get-tuple-element.49.x_ref, bf16[1024,1024]{1,0:T(8,128)(2,1)} %get-tuple-element.55.d_ref.refs_11_, bf16[1024,1024]{1,0:T(8,128)(2,1)} %get-tuple-element.57.dq_ref.refs_7_, bf16[1024,1024]{1,0:T(8,128)(2,1)} %get-tuple-element.58.dk_ref.refs_8_, ...), custom_call_target="tpu_custom_call" | custom-call | flops 6442450944 | bytes 18874368 | tf_op jit(solution)/shard_map/project_backward_1/pallas_call | solution.py:261
  188.3 35.4 %mlp_backward.1 = (bf16[1024,4096]{1,0:T(8,128)(2,1)}, bf16[1024,1024]{1,0:T(8,128)(2,1)}) custom-call(bf16[1024,1024]{1,0:T(8,128)(2,1)} %project_backward_1.1.d_ref.refs_15_, bf16[1024,1024]{1,0:T(8,128)(2,1)} %get-tuple-element.47.h_ref, bf16[1024,4096]{1,0:T(8,128)(2,1)} %get-tuple-element.60.feed_ref, bf16[1024,4096]{1,0:T(8,128)(2,1)} %w1_ref.5, ...), custom_call_target="tpu_custom_call" | custom-call | flops 17179869184 | bytes 33554432 | tf_op jit(solution)/shard_map/mlp_backward/pallas_call | solution.py:199
  223.7 31.0 %attend_backward_0.1 = (bf16[1024,1024]{1,0:T(8,128)(2,1)}, bf16[1024,1024]{1,0:T(8,128)(2,1)}, bf16[1024,1024]{1,0:T(8,128)(2,1)}) custom-call(bf16[1024,1024]{1,0:T(8,128)(2,1)} %get-tuple-element.61.d_ref.refs_5_, bf16[1024,1024]{1,0:T(8,128)(2,1)} %get-tuple-element.44.q_ref, bf16[1024,1024]{1,0:T(8,128)(2,1)} %get-tuple-element.45.k_ref, ...), custom_call_target="tpu_custom_call" | custom-call | flops 4294967296 | bytes 25165824 | tf_op jit(solution)/shard_map/attend_backward_0/pallas_call | solution.py:239
  254.6 444.8 %reduce_gradients.1 = (f32[2,1024,1024]{2,1,0:T(8,128)}, f32[2,1024,1024]{2,1,0:T(8,128)}, f32[2,1024,1024]{2,1,0:T(8,128)}, f32[2,1024,1024]{2,1,0:T(8,128)}, f...) custom-call(bf16[1024,1024]{1,0:T(8,128)(2,1)} %get-tuple-element.43.refs_0_, ...), custom_call_target="tpu_custom_call" | custom-call | flops 51539607552 | bytes 134217728 | tf_op jit(solution)/shard_map/reduce_gradients/pallas_call | solution.py:617
  699.4 15.1 %project_backward_0.1 = bf16[1024,1024]{1,0:T(8,128)(2,1)} custom-call(bf16[1024,1024]{1,0:T(8,128)(2,1)} %bitcast.11, bf16[1024,1024]{1,0:T(8,128)(2,1)} %get-tuple-element.61.d_ref.refs_5_, bf16[1024,1024]{1,0:T(8,128)(2,1)} %get-tuple-element.63.refs_1_.dq_ref, bf16[1024,1024]{1,0:T(8,128)(2,1)} %get-tuple-element.64.refs_2_.dk_ref, ...), custom_call_target="tpu_custom_call" | custom-call | flops 6442450944 | bytes 18874368 | tf_op jit(solution)/shard_map/project_backward_0/pallas_call | solution.py:261
  714.5 0.0 copy-start
  714.5 0.0 slice-start.6
  714.5 8.9 %copy.21 = f32[2,1024,1024]{2,1,0:T(8,128)} copy(f32[2,1024,1024]{2,1,0:T(8,128)} %get-tuple-element.86) | data formatting | bytes 16777216
  723.4 0.0 copy-done
  723.4 0.0 slice-start.7
  723.4 0.0 slice-start.4
  723.4 4.3 copy.22
  727.7 0.0 slice-done.6
  727.7 1.0 slice-done.7
  728.6 0.0 slice-start.5
  728.7 4.3 copy.23
  732.9 0.0 slice-done.4
  732.9 1.4 slice-done.5
  734.4 4.3 copy.24
  738.6 14.1 %copy.25 = f32[1024,4096]{1,0:T(8,128)} copy(f32[1024,4096]{1,0:T(8,128)} %get-tuple-element.90) | data formatting | bytes 33554432
  752.8 0.0 slice-done
  752.8 0.0 slice-done.1
  752.8 0.0 slice-done.2
  752.8 1.3 slice-done.3
  754.1 6.2 copy.26
  (7 shorter events, 0.0 us)
Async XLA Ops:
  714.5 8.9 %copy-start = (f32[2,1024,1024]{2,1,0:T(8,128)S(1)}, f32[2,1024,1024]{2,1,0:T(8,128)}, u32[]{:S(2)}) copy-start(f32[2,1024,1024]{2,1,0:T(8,128)} %get-tuple-element.87) | copy-start | bytes 25165828
  714.5 13.2 %slice-start.6 = ((s8[8388608]{0:T(1024)(128)(4,1)}), s8[4194304]{0:T(1024)(128)(4,1)S(1)}, s32[]{:S(2)}) async-start(s8[8388608]{0:T(1024)(128)(4,1)} %bitcast.7), calls=%async_computation.6 | async-start | bytes 8388608
  723.4 5.2 slice-start.7
  723.4 9.5 %slice-start.4 = ((s8[8388608]{0:T(1024)(128)(4,1)}), s8[4194304]{0:T(1024)(128)(4,1)S(1)}, s32[]{:S(2)}) async-start(s8[8388608]{0:T(1024)(128)(4,1)} %bitcast.5), calls=%async_computation.4 | async-start | bytes 8388608
  728.6 5.7 slice-start.5
  734.4 18.4 %slice-start = ((s8[16777216]{0:T(1024)(128)(4,1)}), s8[4194304]{0:T(1024)(128)(4,1)S(1)}, s32[]{:S(2)}) async-start(s8[16777216]{0:T(1024)(128)(4,1)} %bitcast.3), calls=%async_computation | async-start | bytes 8388608
  734.4 18.4 %slice-start.1 = ((s8[16777216]{0:T(1024)(128)(4,1)}), s8[4194304]{0:T(1024)(128)(4,1)S(1)}, s32[]{:S(2)}) async-start(s8[16777216]{0:T(1024)(128)(4,1)} %bitcast.3), calls=%async_computation.1 | async-start | bytes 8388608
  738.6 14.2 %slice-start.2 = ((s8[16777216]{0:T(1024)(128)(4,1)}), s8[4194304]{0:T(1024)(128)(4,1)S(1)}, s32[]{:S(2)}) async-start(s8[16777216]{0:T(1024)(128)(4,1)} %bitcast.3), calls=%async_computation.2 | async-start | bytes 8388608
  738.6 15.5 %slice-start.3 = ((s8[16777216]{0:T(1024)(128)(4,1)}), s8[4194304]{0:T(1024)(128)(4,1)S(1)}, s32[]{:S(2)}) async-start(s8[16777216]{0:T(1024)(128)(4,1)} %bitcast.3), calls=%async_computation.3 | async-start | bytes 8388608

commit v3 on v2

--- a/solution.py
+++ b/solution.py
@@ -202,6 +202,23 @@
         moved=4 * tokens * ff + 4 * width * ff, name=name)(d_next, hidden, feed, w_up, w_down)
 
 
+def pair_backward(q_pair, k_pair, v_pair, d_pair, low, probs_of):
+    sums = [None] * 3
+    for side in range(2):
+        mask = low if side == 0 else jnp.logical_not(low)
+        d_side = jnp.where(mask, d_pair, 0)
+        probs_16 = probs_of(side)
+        probs_32 = probs_16.astype(jnp.float32)
+        d_probs = dot(d_side, v_pair, 1, 1).astype(jnp.bfloat16).astype(jnp.float32)
+        row_dot = jnp.sum(d_probs * probs_32, axis=-1, keepdims=True)
+        d_scores = (probs_32 * (d_probs - row_dot) * HEAD_DIM ** -0.5).astype(jnp.bfloat16)
+        parts = (dot(d_scores, jnp.where(mask, k_pair, 0), 1, 0),
+                 dot(d_scores, jnp.where(mask, q_pair, 0), 0, 0),
+                 dot(probs_16, d_side, 0, 0))
+        sums = [part if total is None else total + part for total, part in zip(sums, parts)]
+    return sums
+
+
 def attend_backward(d_hidden, query, key_act, value, probs, w_proj, layer, seq):
     tokens, width = d_hidden.shape
     heads = width // HEAD_DIM
@@ -213,19 +230,7 @@
         def pair(j, carry):
             lanes = pl.ds(pl.multiple_of(PAIR * j, PAIR), PAIR)
             q_pair, k_pair, v_pair, d_pair = q_ref[:, lanes], k_ref[:, lanes], v_ref[:, lanes], mix_ref[:, lanes]
-            sums = [None] * 3
-            for side in range(2):
-                mask = low if side == 0 else jnp.logical_not(low)
-                d_side = jnp.where(mask, d_pair, 0)
-                probs_16 = p_ref[2 * j + side]
-                probs_32 = probs_16.astype(jnp.float32)
-                d_probs = dot(d_side, v_pair, 1, 1).astype(jnp.bfloat16).astype(jnp.float32)
-                row_dot = jnp.sum(d_probs * probs_32, axis=-1, keepdims=True)
-                d_scores = (probs_32 * (d_probs - row_dot) * HEAD_DIM ** -0.5).astype(jnp.bfloat16)
-                parts = (dot(d_scores, jnp.where(mask, k_pair, 0), 1, 0),
-                         dot(d_scores, jnp.where(mask, q_pair, 0), 0, 0),
-                         dot(probs_16, d_side, 0, 0))
-                sums = [part if total is None else total + part for total, part in zip(sums, parts)]
+            sums = pair_backward(q_pair, k_pair, v_pair, d_pair, low, lambda side: p_ref[2 * j + side])
             for ref, total in zip((dq_ref, dk_ref, dv_ref), sums):
                 ref[:, lanes] = total.astype(jnp.bfloat16)
             return carry
@@ -307,8 +312,238 @@
     return {"rsz": (rows // 2, 512), "rs1": (rows // 2, 256), "rs2": (rows // 2, 128)}[kind]
 
 
-def reduce_kernel(groups, chunks, n_in, n_out, *refs):
-    ins, outs, scratch = refs[:n_in], refs[n_in:n_in + n_out], refs[n_in + n_out:]
+def between(step, first, count):
+    return jnp.logical_and(step >= first, step < first + count)
+
+
+class Backward:
+    PB_1, MB, AB, PB_0 = 0, 4, 12, 21
+    ROWS = 256
+
+    def __init__(self, at, big, total_buf, w_buf, p_buf, sem, drain):
+        self.at, self.big, self.total, self.w, self.p, self.sem, self.drain = at, big, total_buf, w_buf, p_buf, sem, drain
+        self.tokens, self.width = at["x_0"].shape
+        self.heads = at["probs_0"].shape[1]
+        self.seq = at["probs_0"].shape[2]
+
+    def load(self, name, dest, sem, *index):
+        ref = self.at[name]
+        return pltpu.make_async_copy(ref.at[index] if index else ref, dest, self.sem.at[sem])
+
+    def store(self, src, name, sem, *index):
+        ref = self.at[name]
+        return pltpu.make_async_copy(src, ref.at[index] if index else ref, self.drain.at[sem])
+
+    def row_blocks(self, fn):
+        def body(block, carry):
+            fn(pl.ds(pl.multiple_of(self.ROWS * block, self.ROWS), self.ROWS))
+            return carry
+        lax.fori_loop(0, self.tokens // self.ROWS, body, 0)
+
+    def input_loads(self, layer):
+        spot = 4 if layer else 5
+        copies = [self.load(f"d{kind}_{layer}", self.big.at[i], i) for i, kind in enumerate("qkv")]
+        copies.append(self.load(f"x_{layer}", self.big.at[spot], 3))
+        if layer:
+            copies.append(self.load("dh_1", self.big.at[5], 4))
+        return copies
+
+    def weight_loads(self, layer, block):
+        rows = pl.ds(pl.multiple_of(OUT_BLOCK * block, OUT_BLOCK), OUT_BLOCK)
+        slot = lax.rem(block, 2)
+        return [self.load(name, self.w.at[slot, i], 5 + 3 * slot + i, layer, rows) for i, name in enumerate(("wq", "wk", "wv"))]
+
+    def input_block(self, layer, block):
+        big, blocks = self.big, self.width // OUT_BLOCK
+        slot = lax.rem(block, 2)
+
+        @pl.when(block == 0)
+        def _():
+            for copy in self.input_loads(layer):
+                copy.wait()
+        for copy in self.weight_loads(layer, block):
+            copy.wait()
+
+        @pl.when(block + 1 < blocks)
+        def _():
+            for copy in self.weight_loads(layer, block + 1):
+                copy.start()
+        lanes = pl.ds(pl.multiple_of(OUT_BLOCK * block, OUT_BLOCK), OUT_BLOCK)
+
+        def product(rows):
+            total = dot(big[0, rows], self.w[slot, 0], 1, 1) + dot(big[1, rows], self.w[slot, 1], 1, 1)
+            big[3, rows, lanes] = (total + dot(big[2, rows], self.w[slot, 2], 1, 1)).astype(jnp.bfloat16)
+        self.row_blocks(product)
+
+        @pl.when(block == blocks - 1)
+        def _():
+            x_at, d_at = (4, 5) if layer else (5, 4)
+
+            def close(rows):
+                back = rms_backward(big[x_at, rows].astype(jnp.float32), big[3, rows].astype(jnp.float32))
+                big[3, rows] = (big[d_at, rows].astype(jnp.float32) + back).astype(jnp.bfloat16)
+                if layer:
+                    self.total[rows] = jnp.zeros((self.ROWS, self.width), jnp.float32)
+            self.row_blocks(close)
+            self.store(big.at[3], f"dx_{layer}", 0).start()
+            if layer:
+                self.load("h_0", big.at[4], 3).start()
+                for copy in self.mlp_loads(0):
+                    copy.start()
+
+    def mlp_loads(self, block):
+        slot = lax.rem(block, 2)
+        lanes = pl.ds(pl.multiple_of(FF_BLOCK * block, FF_BLOCK), FF_BLOCK)
+        half = pl.ds(pl.multiple_of(FF_BLOCK * slot, FF_BLOCK), FF_BLOCK)
+        return [self.load("w_up", self.big.at[0, :, half], 5 + 3 * slot, slice(None), lanes),
+                self.load("pre_0", self.big.at[1, :, half], 6 + 3 * slot, slice(None), lanes),
+                self.load("w_down", self.big.at[5, half], 7 + 3 * slot, lanes)]
+
+    def mlp_store(self, block):
+        half = pl.ds(pl.multiple_of(FF_BLOCK * lax.rem(block, 2), FF_BLOCK), FF_BLOCK)
+        lanes = pl.ds(pl.multiple_of(FF_BLOCK * block, FF_BLOCK), FF_BLOCK)
+        return self.store(self.big.at[2, :, half], "dpre_0", 1, slice(None), lanes)
+
+    def mlp_block(self, block):
+        big, blocks = self.big, self.at["w_up"].shape[1] // FF_BLOCK
+
+        @pl.when(block == 0)
+        def _():
+            self.store(big.at[3], "dx_1", 0).wait()
+            self.load("h_0", big.at[4], 3).wait()
+        for copy in self.mlp_loads(block):
+            copy.wait()
+
+        @pl.when(block + 1 < blocks)
+        def _():
+            for copy in self.mlp_loads(block + 1):
+                copy.start()
+
+        @pl.when(block > 0)
+        def _():
+            self.mlp_store(block - 1).wait()
+        half = pl.ds(pl.multiple_of(FF_BLOCK * lax.rem(block, 2), FF_BLOCK), FF_BLOCK)
+
+        def product(rows):
+            d_act = dot(big[3, rows], big[5, half], 1, 1).astype(jnp.bfloat16).astype(jnp.float32)
+            slope = gelu_parts(big[1, rows, half].astype(jnp.float32))[1]
+            d_pre = (d_act * slope).astype(jnp.bfloat16)
+            big[2, rows, half] = d_pre
+            self.total[rows] += dot(d_pre, big[0, :, half], 1, 1)
+        self.row_blocks(product)
+        self.mlp_store(block).start()
+
+        @pl.when(block == blocks - 1)
+        def _():
+            def close(rows):
+                d_normed = self.total[rows].astype(jnp.bfloat16).astype(jnp.float32)
+                back = rms_backward(big[4, rows].astype(jnp.float32), d_normed)
+                big[4, rows] = (big[3, rows].astype(jnp.float32) + back).astype(jnp.bfloat16)
+            self.row_blocks(close)
+            self.store(big.at[4], "dh_0", 2).start()
+            self.load("wo", big.at[0], 4, 0).start()
+            for copy in self.seq_loads(0) + self.probs_loads(0):
+                copy.start()
+
+    def seq_loads(self, seq):
+        rows = pl.ds(pl.multiple_of(self.seq * seq, self.seq), self.seq)
+        return [self.load(f"{kind}_0", self.big.at[1 + lax.rem(seq, 2), pl.ds(self.seq * i, self.seq)], i, rows)
+                for i, kind in enumerate("qkv")]
+
+    def probs_loads(self, piece):
+        half = self.heads // 2
+        heads = pl.ds(half * lax.rem(piece, 2), half)
+        return [self.load("probs_0", self.p.at[lax.rem(piece, 2)], 5 + lax.rem(piece, 2), lax.div(piece, 2), heads)]
+
+    def seq_stores(self, piece):
+        seq, half = lax.div(piece, 2), lax.rem(piece, 2)
+        rows = pl.ds(pl.multiple_of(self.seq * seq, self.seq), self.seq)
+        lanes = pl.ds(pl.multiple_of(self.width // 2 * half, PAIR), self.width // 2)
+        spot = 5 - 2 * lax.rem(seq, 2)
+        return [self.store(self.big.at[spot, pl.ds(self.seq * i, self.seq), lanes], f"d{kind}_0", 3 + i, rows, lanes)
+                for i, kind in enumerate("qkv")]
+
+    def attention_piece(self, piece):
+        big, pieces = self.big, 2 * (self.tokens // self.seq)
+        seq, half = lax.div(piece, 2), lax.rem(piece, 2)
+        spot, out = 1 + lax.rem(seq, 2), 5 - 2 * lax.rem(seq, 2)
+
+        @pl.when(piece == 0)
+        def _():
+            self.mlp_store(self.at["w_up"].shape[1] // FF_BLOCK - 1).wait()
+            self.store(big.at[4], "dh_0", 2).wait()
+            self.load("wo", big.at[0], 4, 0).wait()
+
+        @pl.when(piece > 0)
+        def _():
+            for copy in self.seq_stores(piece - 1):
+                copy.wait()
+        for copy in self.probs_loads(piece):
+            copy.wait()
+
+        @pl.when(piece + 1 < pieces)
+        def _():
+            for copy in self.probs_loads(piece + 1):
+                copy.start()
+        mixed = pl.ds(3 * self.seq, self.seq)
+
+        @pl.when(half == 0)
+        def _():
+            for copy in self.seq_loads(seq):
+                copy.wait()
+
+            @pl.when(piece + 2 < pieces)
+            def _():
+                for copy in self.seq_loads(seq + 1):
+                    copy.start()
+            rows = pl.ds(pl.multiple_of(self.seq * seq, self.seq), self.seq)
+            big[spot, mixed] = dot(big[4, rows], big[0], 1, 1).astype(jnp.bfloat16)
+        low = lax.broadcasted_iota(jnp.int32, (self.seq, PAIR), 1) < HEAD_DIM
+        pairs = self.heads // 4
+
+        def pair(j, carry):
+            lanes = pl.ds(pl.multiple_of(PAIR * (pairs * half + j), PAIR), PAIR)
+            q_pair, k_pair, v_pair, d_pair = (big[spot, pl.ds(self.seq * i, self.seq), lanes] for i in range(4))
+            for i, total in enumerate(pair_backward(q_pair, k_pair, v_pair, d_pair, low, lambda side: self.p[half, 2 * j + side])):
+                big[out, pl.ds(self.seq * i, self.seq), lanes] = total.astype(jnp.bfloat16)
+            return carry
+        lax.fori_loop(0, pairs, pair, 0)
+        for copy in self.seq_stores(piece):
+            copy.start()
+
+    def item(self, step):
+        blocks = self.width // OUT_BLOCK
+        pieces = 2 * (self.tokens // self.seq)
+
+        @pl.when(step == self.PB_1)
+        def _():
+            for copy in self.input_loads(1) + self.weight_loads(1, 0):
+                copy.start()
+        pl.when(between(step, self.PB_1, blocks))(lambda: self.input_block(1, step - self.PB_1))
+        pl.when(between(step, self.MB, 8))(lambda: self.mlp_block(step - self.MB))
+        pl.when(between(step, self.AB, pieces))(lambda: self.attention_piece(step - self.AB))
+
+        @pl.when(step == self.PB_0 - 1)
+        def _():
+            for copy in self.seq_stores(pieces - 1):
+                copy.wait()
+            for copy in self.input_loads(0) + self.weight_loads(0, 0):
+                copy.start()
+        pl.when(between(step, self.PB_0, blocks))(lambda: self.input_block(0, step - self.PB_0))
+
+        @pl.when(step == self.PB_0 + blocks)
+        def _():
+            self.store(self.big.at[3], "dx_0", 0).wait()
+
+
+def finish_kernel(groups, chunks, in_names, out_names, remote, *refs):
+    names = [*in_names, *out_names]
+    at, scratch = dict(zip(names, refs[:len(names)])), refs[len(names):]
+    (big, total_buf, w_buf, p_buf, item_sem, drain_sem), scratch = scratch[:6], scratch[6:]
+    backward = Backward(at, big, total_buf, w_buf, p_buf, item_sem, drain_sem)
+    if not remote:
+        lax.fori_loop(0, chunks + WRITE_AT + 1, lambda step, carry: backward.item(step) or carry, 0)
+        return
     (lhs_buf, rhs_buf, own, part, part_in, gath), scratch = scratch[:6], scratch[6:]
     land_keys = [key for key, st in enumerate(STAGES) if st[1].startswith("rs")]
     landing = dict(zip(land_keys, scratch[:len(land_keys)]))
@@ -427,7 +662,7 @@
 
     def out_copies(half, group, local, whose):
         out, layer = group["out"]
-        ref = outs[out] if layer is None else outs[out].at[layer]
+        ref = at[out] if layer is None else at[out].at[layer]
         rows, cols = group["place"](local)
         first = pl.multiple_of(rows + CORE_ROWS * whose + half * SET_ROWS, SET_ROWS)
         return ref.at[pl.ds(first, SET_ROWS), pl.ds(pl.multiple_of(cols, 128), LANES)]
@@ -448,10 +683,10 @@
             for whose in (0, 1):
                 first = rows + CORE_ROWS * (core if whose == 0 else 1 - core)
                 copies.append(pltpu.make_async_copy(
-                    ins[lhs].at[:, pl.ds(pl.multiple_of(first, CORE_ROWS), CORE_ROWS)],
+                    at[lhs].at[:, pl.ds(pl.multiple_of(first, CORE_ROWS), CORE_ROWS)],
                     lhs_buf.at[slot, app, whose], load_sem.at[slot, app, whose]))
             copies.append(pltpu.make_async_copy(
-                ins[rhs].at[:, pl.ds(pl.multiple_of(cols, 128), LANES)], rhs_buf.at[slot, app], load_sem.at[slot, app, 2]))
+                at[rhs].at[:, pl.ds(pl.multiple_of(cols, 128), LANES)], rhs_buf.at[slot, app], load_sem.at[slot, app, 2]))
         return copies
 
     def for_group(chunk, fn):
@@ -587,44 +822,60 @@
         def _():
             pair_copy(1, lax.rem(step, 2)).start()
 
+        backward.item(step)
         return carry
 
     lax.fori_loop(0, last + 1, round_, 0)
 
 
-def reduce_gradients(operands, groups, chunks, out_shapes, tokens, collective_id=0):
+def finish_backward(inputs, groups, chunks, weights, tokens, seq, collective_id=0, remote=True):
+    width, ff = inputs["w_up"].shape
     landing = [pltpu.VMEM((2,) + piece_shape(st[0], st[1]), jnp.float32) for st in STAGES if st[1].startswith("rs")]
-    apps = max(len(g["lhs"]) for g in groups)
+    apps = 2
+    outs = {name: jax.ShapeDtypeStruct(shape, jnp.float32) for name, shape in weights.items()}
+    for name in ("dx_0", "dx_1", "dh_0", "dq_0", "dk_0", "dv_0"):
+        outs[name] = bf16(tokens, width)
+    outs["dpre_0"] = bf16(tokens, ff)
+    heads = width // HEAD_DIM
     scratch = [
-        pltpu.VMEM((2, apps, 2, tokens, CORE_ROWS), jnp.bfloat16),
-        pltpu.VMEM((2, apps, tokens, LANES), jnp.bfloat16),
-        pltpu.VMEM((OWN_SLOTS, CORE_ROWS, LANES), jnp.float32),
-        pltpu.VMEM((2, CORE_ROWS, LANES), jnp.float32),
-        pltpu.VMEM((2, CORE_ROWS, LANES), jnp.float32),
-        pltpu.VMEM((AG_SLOTS, CORE_ROWS, LANES), jnp.float32),
-        *landing,
-        pltpu.SemaphoreType.DMA((2, apps, 3)),
-        pltpu.SemaphoreType.DMA((len(STAGES),)),
-        pltpu.SemaphoreType.DMA((len(STAGES), 2)),
-        pltpu.SemaphoreType.DMA((2,)),
-        pltpu.SemaphoreType.DMA((2, 2)),
-        pltpu.SemaphoreType.DMA((2,)),
-        pltpu.SemaphoreType.DMA((2,)),
-        pltpu.SemaphoreType.DMA((2, 2)),
-        pltpu.SemaphoreType.REGULAR((2, 5)),
+        pltpu.VMEM((6, tokens, width), jnp.bfloat16),
+        pltpu.VMEM((tokens, width), jnp.float32),
+        pltpu.VMEM((2, 3, OUT_BLOCK, width), jnp.bfloat16),
+        pltpu.VMEM((2, heads // 2, seq, seq), jnp.bfloat16),
+        pltpu.SemaphoreType.DMA((11,)),
+        pltpu.SemaphoreType.DMA((6,)),
     ]
-    flops = sum(2 * g["count"] * len(g["lhs"]) * TILE_ROWS * LANES * tokens for g in groups)
-    return pl.pallas_call(
-        functools.partial(reduce_kernel, groups, chunks, len(operands), len(out_shapes)),
-        out_shape=[jax.ShapeDtypeStruct(shape, jnp.float32) for shape in out_shapes],
-        in_specs=[pl.BlockSpec(memory_space=pl.ANY)] * len(operands),
-        out_specs=[pl.BlockSpec(memory_space=pl.ANY)] * len(out_shapes),
+    if remote:
+        scratch += [
+            pltpu.VMEM((2, apps, 2, tokens, CORE_ROWS), jnp.bfloat16),
+            pltpu.VMEM((2, apps, tokens, LANES), jnp.bfloat16),
+            pltpu.VMEM((OWN_SLOTS, CORE_ROWS, LANES), jnp.float32),
+            pltpu.VMEM((2, CORE_ROWS, LANES), jnp.float32),
+            pltpu.VMEM((2, CORE_ROWS, LANES), jnp.float32),
+            pltpu.VMEM((AG_SLOTS, CORE_ROWS, LANES), jnp.float32),
+            *landing,
+            pltpu.SemaphoreType.DMA((2, apps, 3)),
+            pltpu.SemaphoreType.DMA((len(STAGES),)),
+            pltpu.SemaphoreType.DMA((len(STAGES), 2)),
+            pltpu.SemaphoreType.DMA((2,)),
+            pltpu.SemaphoreType.DMA((2, 2)),
+            pltpu.SemaphoreType.DMA((2,)),
+            pltpu.SemaphoreType.DMA((2,)),
+            pltpu.SemaphoreType.DMA((2, 2)),
+            pltpu.SemaphoreType.REGULAR((2, 5)),
+        ]
+    params = dict(collective_id=collective_id, has_side_effects=True) if remote else {}
+    results = pl.pallas_call(
+        functools.partial(finish_kernel, groups, chunks, list(inputs), list(outs), remote),
+        out_shape=list(outs.values()),
+        in_specs=[pl.BlockSpec(memory_space=pl.ANY)] * len(inputs),
+        out_specs=[pl.BlockSpec(memory_space=pl.ANY)] * len(outs),
         scratch_shapes=scratch,
-        compiler_params=pltpu.CompilerParams(
-            collective_id=collective_id, has_side_effects=True, vmem_limit_bytes=60 * 1024 * 1024),
-        cost_estimate=pl.CostEstimate(flops=flops, bytes_accessed=128 * 1024 * 1024, transcendentals=0),
-        name="reduce_gradients",
-    )(*operands)
+        compiler_params=pltpu.CompilerParams(vmem_limit_bytes=67_043_328, **params),
+        cost_estimate=pl.CostEstimate(flops=20 * tokens * width * ff, bytes_accessed=256 * MIB, transcendentals=0),
+        name="finish_backward",
+    )(*inputs.values())
+    return dict(zip(outs, results))
 
 
 def gradient_groups(width, ff):
@@ -641,51 +892,42 @@
         return TILE_ROWS * lax.rem(local, width // TILE_ROWS), LANES * lax.div(local, width // TILE_ROWS)
 
     def attention(layer):
-        base = 6 * layer
-        for out in range(3):
-            add(width // TILE_ROWS, [base], [base + 1 + out], (out, layer), tall)
-        add(width // TILE_ROWS, [base + 4], [base + 5], (3, layer), tall)
+        for out, kind in enumerate("qkv"):
+            add(width // TILE_ROWS, [f"u_{layer}"], [f"d{kind}_{layer}"], (f"g_{kind}", layer), tall)
+        add(width // TILE_ROWS, [f"mixed_{layer}"], [f"dh_{layer}"], ("g_o", layer), tall)
 
     attention(1)
-    add(ff // TILE_ROWS, [14, 18], [15, 19], (5, None), tall)
-    add(ff // TILE_ROWS, [12, 16], [13, 17], (4, None), wide)
+    add(ff // TILE_ROWS, ["act_0", "act_1"], ["dx_1", "cot"], ("g_down", None), tall)
+    add(ff // TILE_ROWS, ["n_0", "n_1"], ["dpre_0", "dpre_1"], ("g_up", None), wide)
     attention(0)
     return groups, sum(group["count"] for group in groups)
 
 
 def local_operands(x_init, cot_out, w_query, w_key, w_value, w_proj, w_up, w_down):
     batch, seq, width = x_init.shape
-    x_in = [x_init.reshape(batch * seq, width), None]
-    d_act = cot_out.reshape(batch * seq, width)
-    kept = []
+    tokens = batch * seq
+    at = {"x_0": x_init.reshape(tokens, width), "cot": cot_out.reshape(tokens, width)}
     for layer in (0, 1):
-        normed, query, key_act, value = project_qkv(x_in[layer], w_query, w_key, w_value, layer)
-        probs, mixed, hidden, normed2 = attend(x_in[layer], query, key_act, value, w_proj, layer, seq)
-        kept.append((normed, query, key_act, value, probs, mixed, hidden, normed2))
+        x_in = at[f"x_{layer}"]
+        at[f"u_{layer}"], query, key_act, value = project_qkv(x_in, w_query, w_key, w_value, layer)
+        probs, at[f"mixed_{layer}"], hidden, at[f"n_{layer}"] = attend(x_in, query, key_act, value, w_proj, layer, seq)
         if layer == 0:
-            pre_act, act_0, x_in[1] = mlp_forward(hidden, normed2, w_up, w_down)
-    attn, mlp = [None, None], [None, None]
-    for layer in (1, 0):
-        normed, query, key_act, value, probs, mixed, hidden, normed2 = kept[layer]
-        if layer == 1:
-            d_pre, d_hidden, act = mlp_backward(d_act, hidden, normed2, w_up, w_down, True, "mlp_both")
-        else:
-            d_pre, d_hidden = mlp_backward(d_act, hidden, pre_act, w_up, w_down, False, "mlp_backward")
-            act = act_0
-        mlp[layer] = (normed2, d_pre, act, d_act)
-        d_query, d_key, d_value = attend_backward(d_hidden, query, key_act, value, probs, w_proj, layer, seq)
-        d_act = project_backward(x_in[layer], d_hidden, d_query, d_key, d_value, w_query, w_key, w_value, layer)
-        attn[layer] = (normed, d_query, d_key, d_value, mixed, d_hidden)
-    return [*attn[0], *attn[1], *mlp[0], *mlp[1]], d_act.reshape(batch, seq, width)
+            at.update(q_0=query, k_0=key_act, v_0=value, probs_0=probs, h_0=hidden)
+            at["pre_0"], at["act_0"], at["x_1"] = mlp_forward(hidden, at["n_0"], w_up, w_down)
+    at["dpre_1"], at["dh_1"], at["act_1"] = mlp_backward(at["cot"], hidden, at["n_1"], w_up, w_down, True, "mlp_both")
+    at["dq_1"], at["dk_1"], at["dv_1"] = attend_backward(at["dh_1"], query, key_act, value, probs, w_proj, 1, seq)
+    at.update(wq=w_query, wk=w_key, wv=w_value, wo=w_proj, w_up=w_up, w_down=w_down)
+    return at
 
 
 def solution(mesh):
     def local_step(x_init, cot_out, w_query, w_key, w_value, w_proj, w_up, w_down):
-        operands, d_init = local_operands(x_init, cot_out, w_query, w_key, w_value, w_proj, w_up, w_down)
-        groups, chunks = gradient_groups(x_init.shape[2], w_up.shape[1])
-        shapes = [w_query.shape, w_key.shape, w_value.shape, w_proj.shape, w_up.shape, w_down.shape]
-        grads = reduce_gradients(operands, groups, chunks, shapes, operands[0].shape[0])
-        return (*grads, d_init)
+        batch, seq, width = x_init.shape
+        inputs = local_operands(x_init, cot_out, w_query, w_key, w_value, w_proj, w_up, w_down)
+        groups, chunks = gradient_groups(width, w_up.shape[1])
+        weights = dict(g_q=w_query.shape, g_k=w_key.shape, g_v=w_value.shape, g_o=w_proj.shape, g_up=w_up.shape, g_down=w_down.shape)
+        res = finish_backward(inputs, groups, chunks, weights, batch * seq, seq)
+        return (*(res[name] for name in weights), res["dx_0"].reshape(x_init.shape))
 
     data_spec = P("data")
     full_spec = P()

time: 761 us -> 672 us (0.88)
  Pallas kernels: 714 us -> 624 us
    pallas_call x2 -> x1, Pallas kernels: 74.1 us -> 38.7 us  [mlp_backward(): call(kernel, (steps,), [full, full, full if replay else wide, up, down],...]
    pallas_call x2 -> x1, Pallas kernels: 61.8 us -> 30.8 us  [attend_backward(): call(kernel, (tokens // seq,), [row, row, row, row, block, weight], [act,...]
    pallas_call x3 -> x1, Pallas kernels: 475 us -> 451 us  [finish_backward(): pl.pallas_call(functools.partial(finish_kernel, groups, chunks, list(inpu...]
    unnamed x24 -> x27, local copies, waits for them, and re-layouts: 45.7 us -> 47.2 us
where the time goes in v3:
time: 672 us; the launch traced here: 671 us
  Pallas kernels  624 us (93%)
  local copies, waits for them, and re-layouts  47.2 us (7%)
    pallas_call x1, Pallas kernels, finish_backward(): pl.pallas_call(functools.partial(finish_kernel, groups, chunks, list(inpu...  451 us
    pallas_call x2, Pallas kernels, attend(): call(kernel, (tokens // seq,), [row, row, row, row, weight], [(bf16(token...  49.6 us
    unnamed x27, local copies, waits for them, and re-layouts  47.2 us
    pallas_call x1, Pallas kernels, mlp_backward(): call(kernel, (steps,), [full, full, full if replay else wide, up, down],...  38.7 us
    pallas_call x1, Pallas kernels, attend_backward(): call(kernel, (tokens // seq,), [row, row, row, row, block, weight], [act,...  30.8 us
    pallas_call x1, Pallas kernels, mlp_forward(): call(kernel, (steps,), [full, full, up, down], [(bf16(tokens, ff), wide),...  30.4 us
    pallas_call x2, Pallas kernels, project_qkv(): call(kernel, (width // OUT_BLOCK,), [whole((tokens, width)), weight, weig...  22.7 us

profile of v3, /device:TPU:0, one launch (start us, length us, event | category | flops | bytes accessed | tf_op | source)
XLA Modules:
  0.0 671.4 jit_solution(2883397109524042966)
XLA Ops:
  0.6 11.4 %qkv_0.1 = (bf16[1024,1024]{1,0:T(8,128)(2,1)}, bf16[1024,1024]{1,0:T(8,128)(2,1)}, bf16[1024,1024]{1,0:T(8,128)(2,1)}, bf16[1024,1024]{1,0:T(8,128)(2,1)}) custom-call(bf16[1024,1024]{1,0:T(8,128)(2,1)} %bitcast.10, bf16[2,1024,1024]{2,1,0:T(8,128)(2,1)} %refs_22_.1, bf16[2,1024,1024]{2,1,0:T(8,128)(2,1)} %refs_23_.1, bf16[2,1024,1024]{2,1,0:T(8,128)(2,1)} %refs_24_.1), custom_call_target="tpu_custom_call" | custom-call | flops 6442450944 | bytes 14680064 | tf_op jit(solution)/shard_map/qkv_0/pallas_call | solution.py:77
  12.0 24.8 %attend_0.1 = (bf16[4,16,256,256]{3,2,1,0:T(8,128)(2,1)}, bf16[1024,1024]{1,0:T(8,128)(2,1)}, bf16[1024,1024]{1,0:T(8,128)(2,1)}, bf16[1024,1024]{1,0:T(8,128)(2,1)}) custom-call(bf16[1024,1024]{1,0:T(8,128)(2,1)} %bitcast.11, bf16[1024,1024]{1,0:T(8,128)(2,1)} %get-tuple-element.40.q_ref.refs_5_, bf16[1024,1024]{1,0:T(8,128)(2,1)} %get-tuple-element.41.k_ref.refs_6_, ...), custom_call_target="tpu_custom_call" | custom-call | flops 3221225472 | bytes 20971520 | tf_op jit(solution)/shard_map/attend_0/pallas_call | solution.py:117
  36.8 30.4 %mlp_forward.1 = (bf16[1024,4096]{1,0:T(8,128)(2,1)}, bf16[1024,4096]{1,0:T(8,128)(2,1)}, bf16[1024,1024]{1,0:T(8,128)(2,1)}) custom-call(bf16[1024,1024]{1,0:T(8,128)(2,1)} %get-tuple-element.46.h_ref.refs_9_, bf16[1024,1024]{1,0:T(8,128)(2,1)} %get-tuple-element.44.n_ref.refs_4_, bf16[1024,4096]{1,0:T(8,128)(2,1)} %refs_26_.1, bf16[4096,1024]{1,0:T(8,128)(2,1)} %refs_27_.1), custom_call_target="tpu_custom_call" | custom-call | flops 17179869184 | bytes 33554432 | tf_op jit(solution)/shard_map/mlp_forward/pallas_call | solution.py:153
  67.2 11.4 %qkv_1.1 = (bf16[1024,1024]{1,0:T(8,128)(2,1)}, bf16[1024,1024]{1,0:T(8,128)(2,1)}, bf16[1024,1024]{1,0:T(8,128)(2,1)}, bf16[1024,1024]{1,0:T(8,128)(2,1)}) custom-call(bf16[1024,1024]{1,0:T(8,128)(2,1)} %get-tuple-element.49.x_ref.refs_12_, bf16[2,1024,1024]{2,1,0:T(8,128)(2,1)} %refs_22_.1, bf16[2,1024,1024]{2,1,0:T(8,128)(2,1)} %refs_23_.1, ...), custom_call_target="tpu_custom_call" | custom-call | flops 6442450944 | bytes 14680064 | tf_op jit(solution)/shard_map/qkv_1/pallas_call | solution.py:77
  78.5 24.8 %attend_1.1 = (bf16[4,16,256,256]{3,2,1,0:T(8,128)(2,1)}, bf16[1024,1024]{1,0:T(8,128)(2,1)}, bf16[1024,1024]{1,0:T(8,128)(2,1)}, bf16[1024,1024]{1,0:T(8,128)(2,1)}) custom-call(bf16[1024,1024]{1,0:T(8,128)(2,1)} %get-tuple-element.49.x_ref.refs_12_, bf16[1024,1024]{1,0:T(8,128)(2,1)} %get-tuple-element.51.q_ref, ...), custom_call_target="tpu_custom_call" | custom-call | flops 3221225472 | bytes 20971520 | tf_op jit(solution)/shard_map/attend_1/pallas_call | solution.py:117
  103.4 38.7 %mlp_both.1 = (bf16[1024,4096]{1,0:T(8,128)(2,1)}, bf16[1024,1024]{1,0:T(8,128)(2,1)}, bf16[1024,4096]{1,0:T(8,128)(2,1)}) custom-call(bf16[1024,1024]{1,0:T(8,128)(2,1)} %bitcast.13, bf16[1024,1024]{1,0:T(8,128)(2,1)} %get-tuple-element.56.h_ref, bf16[1024,1024]{1,0:T(8,128)(2,1)} %get-tuple-element.55.feed_ref.refs_15_, bf16[1024,4096]{1,0:T(8,128)(2,1)} %refs_26_.1, ...), custom_call_target="tpu_custom_call" | custom-call | flops 25769803776 | bytes 33554432 | tf_op jit(solution)/shard_map/mlp_both/pallas_call | solution.py:199
  142.1 30.8 %attend_backward_1.1 = (bf16[1024,1024]{1,0:T(8,128)(2,1)}, bf16[1024,1024]{1,0:T(8,128)(2,1)}, bf16[1024,1024]{1,0:T(8,128)(2,1)}) custom-call(bf16[1024,1024]{1,0:T(8,128)(2,1)} %get-tuple-element.58.d_ref.refs_17_, bf16[1024,1024]{1,0:T(8,128)(2,1)} %get-tuple-element.51.q_ref, bf16[1024,1024]{1,0:T(8,128)(2,1)} %get-tuple-element.52.k_ref, ...), custom_call_target="tpu_custom_call" | custom-call | flops 4294967296 | bytes 25165824 | tf_op jit(solution)/shard_map/attend_backward_1/pallas_call | solution.py:244
  172.9 451.3 %finish_backward.1 = (f32[2,1024,1024]{2,1,0:T(8,128)}, f32[2,1024,1024]{2,1,0:T(8,128)}, f32[2,1024,1024]{2,1,0:T(8,128)}, f32[2,1024,1024]{2,1,0:T(8,128)}, f3...) custom-call(bf16[1024,1024]{1,0:T(8,128)(2,1)} %bitcast.12, ...), custom_call_target="tpu_custom_call" | custom-call | flops 85899345920 | bytes 268435456 | tf_op jit(solution)/shard_map/finish_backward/pallas_call | solution.py:868
  624.2 0.0 copy-start
  624.2 0.0 slice-start.6
  624.2 8.9 %copy.22 = f32[2,1024,1024]{2,1,0:T(8,128)} copy(f32[2,1024,1024]{2,1,0:T(8,128)} %get-tuple-element.78) | data formatting | bytes 16777216
  633.1 0.0 copy-done
  633.1 0.0 slice-start.7
  633.1 0.0 slice-start.4
  633.1 4.3 copy.23
  637.4 0.0 slice-done.6
  637.4 1.0 slice-done.7
  638.3 0.0 slice-start.5
  638.3 4.3 copy.24
  642.6 0.0 slice-done.4
  642.6 1.4 slice-done.5
  644.1 0.0 slice-start
  644.1 0.0 slice-start.1
  644.1 4.3 copy.25
  648.3 14.1 %copy.26 = f32[1024,4096]{1,0:T(8,128)} copy(f32[1024,4096]{1,0:T(8,128)} %get-tuple-element.82) | data formatting | bytes 33554432
  662.5 0.0 slice-done
  662.5 0.0 slice-done.1
  662.5 0.0 slice-done.2
  662.5 1.3 slice-done.3
  663.8 6.3 copy.27
  670.1 0.0 copy-done.1
  670.1 1.3 copy.28
  (6 shorter events, 0.0 us)
Async XLA Ops:
  624.2 8.9 %copy-start = (f32[2,1024,1024]{2,1,0:T(8,128)S(1)}, f32[2,1024,1024]{2,1,0:T(8,128)}, u32[]{:S(2)}) copy-start(f32[2,1024,1024]{2,1,0:T(8,128)} %get-tuple-element.79) | copy-start | bytes 25165828
  624.2 13.1 %slice-start.6 = ((s8[8388608]{0:T(1024)(128)(4,1)}), s8[4194304]{0:T(1024)(128)(4,1)S(1)}, s32[]{:S(2)}) async-start(s8[8388608]{0:T(1024)(128)(4,1)} %bitcast.7), calls=%async_computation.6 | async-start | bytes 8388608
  633.1 5.2 slice-start.7
  633.1 9.5 %slice-start.4 = ((s8[8388608]{0:T(1024)(128)(4,1)}), s8[4194304]{0:T(1024)(128)(4,1)S(1)}, s32[]{:S(2)}) async-start(s8[8388608]{0:T(1024)(128)(4,1)} %bitcast.5), calls=%async_computation.4 | async-start | bytes 8388608
  638.3 5.7 slice-start.5
  644.1 18.4 %slice-start = ((s8[16777216]{0:T(1024)(128)(4,1)}), s8[4194304]{0:T(1024)(128)(4,1)S(1)}, s32[]{:S(2)}) async-start(s8[16777216]{0:T(1024)(128)(4,1)} %bitcast.3), calls=%async_computation | async-start | bytes 8388608
  644.1 18.4 %slice-start.1 = ((s8[16777216]{0:T(1024)(128)(4,1)}), s8[4194304]{0:T(1024)(128)(4,1)S(1)}, s32[]{:S(2)}) async-start(s8[16777216]{0:T(1024)(128)(4,1)} %bitcast.3), calls=%async_computation.1 | async-start | bytes 8388608
  648.3 14.2 %slice-start.2 = ((s8[16777216]{0:T(1024)(128)(4,1)}), s8[4194304]{0:T(1024)(128)(4,1)S(1)}, s32[]{:S(2)}) async-start(s8[16777216]{0:T(1024)(128)(4,1)} %bitcast.3), calls=%async_computation.2 | async-start | bytes 8388608
  648.3 15.5 %slice-start.3 = ((s8[16777216]{0:T(1024)(128)(4,1)}), s8[4194304]{0:T(1024)(128)(4,1)S(1)}, s32[]{:S(2)}) async-start(s8[16777216]{0:T(1024)(128)(4,1)} %bitcast.3), calls=%async_computation.3 | async-start | bytes 8388608
  663.8 6.3 copy-start.1

commit v4 on v3

--- a/solution.py
+++ b/solution.py
@@ -14,6 +14,7 @@
 OUT_BLOCK = 256
 GELU_A = (2.0 / 3.141592653589793) ** 0.5
 GELU_B = 0.044715
+SOFTMAX_SCALE = HEAD_DIM ** -0.5 * 1.4426950408889634
 MIB = 1024 * 1024
 
 
@@ -39,167 +40,8 @@
     return pre * half, slope
 
 
-def call(kernel, grid, in_specs, outs, scratch=(), flops=0, moved=0, name=None):
-    return pl.pallas_call(
-        kernel,
-        grid=grid,
-        in_specs=in_specs,
-        out_specs=[spec for _, spec in outs],
-        out_shape=[shape for shape, _ in outs],
-        scratch_shapes=list(scratch),
-        compiler_params=pltpu.CompilerParams(vmem_limit_bytes=60 * MIB, dimension_semantics=("arbitrary",) * len(grid)),
-        cost_estimate=pl.CostEstimate(flops=flops, bytes_accessed=moved, transcendentals=0),
-        name=name,
-    )
-
-
-def whole(shape):
-    return pl.BlockSpec(shape, lambda *_: (0,) * len(shape), pipeline_mode=pl.Buffered(1))
-
-
 def bf16(*shape):
     return jax.ShapeDtypeStruct(shape, jnp.bfloat16)
-
-
-def project_qkv(x_act, w_query, w_key, w_value, layer):
-    tokens, width = x_act.shape
-
-    def kernel(x_ref, wq_ref, wk_ref, wv_ref, u_ref, q_ref, k_ref, v_ref):
-        @pl.when(pl.program_id(0) == 0)
-        def _():
-            u_ref[...] = rms_norm(x_ref[...].astype(jnp.float32)).astype(jnp.bfloat16)
-
-        for w_ref, o_ref in ((wq_ref, q_ref), (wk_ref, k_ref), (wv_ref, v_ref)):
-            o_ref[...] = dot(u_ref[...], w_ref[...], 1, 0).astype(jnp.bfloat16)
-
-    weight = pl.BlockSpec((None, width, OUT_BLOCK), lambda i: (layer, 0, i))
-    block = pl.BlockSpec((tokens, OUT_BLOCK), lambda i: (0, i))
-    return call(
-        kernel, (width // OUT_BLOCK,), [whole((tokens, width)), weight, weight, weight],
-        [(bf16(tokens, width), whole((tokens, width)))] + [(bf16(tokens, width), block)] * 3,
-        flops=6 * tokens * width * width, moved=14 * tokens * width, name=f"qkv_{layer}")(x_act, w_query, w_key, w_value)
-
-
-def attend(x_act, query, key_act, value, w_proj, layer, seq):
-    tokens, width = x_act.shape
-    heads = width // HEAD_DIM
-
-    def kernel(x_ref, q_ref, k_ref, v_ref, wo_ref, p_ref, mix_ref, h_ref, n_ref):
-        low = lax.broadcasted_iota(jnp.int32, (seq, PAIR), 1) < HEAD_DIM
-
-        def pair(j, carry):
-            lanes = pl.ds(pl.multiple_of(PAIR * j, PAIR), PAIR)
-            q_pair, k_pair, v_pair = q_ref[:, lanes], k_ref[:, lanes], v_ref[:, lanes]
-            total = None
-            for side in range(2):
-                mask = low if side == 0 else jnp.logical_not(low)
-                scores = dot(jnp.where(mask, q_pair, 0), k_pair, 1, 1) * HEAD_DIM ** -0.5
-                top = jnp.max(scores, axis=-1, keepdims=True)
-                raised = jnp.exp(scores - top)
-                inverse = 1.0 / jnp.sum(raised, axis=-1, keepdims=True)
-                probs = (raised * inverse).astype(jnp.bfloat16)
-                p_ref[2 * j + side] = probs
-                part = dot(probs, jnp.where(mask, v_pair, 0), 1, 0)
-                total = part if total is None else total + part
-            mix_ref[:, lanes] = total.astype(jnp.bfloat16)
-            return carry
-
-        lax.fori_loop(0, heads // 2, pair, 0)
-        attn = dot(mix_ref[...], wo_ref[...], 1, 0).astype(jnp.bfloat16)
-        hidden = (x_ref[...].astype(jnp.float32) + attn.astype(jnp.float32)).astype(jnp.bfloat16)
-        h_ref[...] = hidden
-        n_ref[...] = rms_norm(hidden.astype(jnp.float32)).astype(jnp.bfloat16)
-
-    row = pl.BlockSpec((seq, width), lambda i: (i, 0))
-    weight = pl.BlockSpec((None, width, width), lambda i: (layer, 0, 0), pipeline_mode=pl.Buffered(1))
-    probs = pl.BlockSpec((None, heads, seq, seq), lambda i: (i, 0, 0, 0))
-    act = (bf16(tokens, width), row)
-    return call(
-        kernel, (tokens // seq,), [row, row, row, row, weight], [(bf16(tokens // seq, heads, seq, seq), probs), act, act, act],
-        flops=2 * tokens * width * (width + 2 * seq), moved=20 * tokens * width, name=f"attend_{layer}",
-    )(x_act, query, key_act, value, w_proj)
-
-
-def mlp_forward(hidden, normed2, w_up, w_down):
-    tokens, width = hidden.shape
-    ff = w_up.shape[1]
-    steps = ff // FF_BLOCK
-
-    def kernel(h_ref, n_ref, w1_ref, w2_ref, pre_ref, act_ref, x_ref, acc_ref):
-        i = pl.program_id(0)
-        pre = dot(n_ref[...], w1_ref[...], 1, 0).astype(jnp.bfloat16)
-        pre_ref[...] = pre
-        act = gelu_parts(pre.astype(jnp.float32))[0].astype(jnp.bfloat16)
-        act_ref[...] = act
-        part = dot(act, w2_ref[...], 1, 0)
-
-        @pl.when(i == 0)
-        def _():
-            acc_ref[...] = part
-
-        @pl.when(i > 0)
-        def _():
-            acc_ref[...] += part
-
-        @pl.when(i == steps - 1)
-        def _():
-            out = acc_ref[...].astype(jnp.bfloat16).astype(jnp.float32)
-            x_ref[...] = (h_ref[...].astype(jnp.float32) + out).astype(jnp.bfloat16)
-
-    full = whole((tokens, width))
-    up = pl.BlockSpec((width, FF_BLOCK), lambda i: (0, i))
-    down = pl.BlockSpec((FF_BLOCK, width), lambda i: (i, 0))
-    wide = pl.BlockSpec((tokens, FF_BLOCK), lambda i: (0, i))
-    return call(
-        kernel, (steps,), [full, full, up, down],
-        [(bf16(tokens, ff), wide), (bf16(tokens, ff), wide), (bf16(tokens, width), full)],
-        [pltpu.VMEM((tokens, width), jnp.float32)], flops=4 * tokens * width * ff, moved=4 * tokens * ff + 4 * width * ff,
-        name="mlp_forward")(hidden, normed2, w_up, w_down)
-
-
-def mlp_backward(d_next, hidden, feed, w_up, w_down, replay, name):
-    tokens, width = hidden.shape
-    ff = w_up.shape[1]
-    steps = ff // FF_BLOCK
-
-    def kernel(d_ref, h_ref, feed_ref, w1_ref, w2_ref, *refs):
-        outs, acc_ref = refs[:-1], refs[-1]
-        i = pl.program_id(0)
-        if replay:
-            pre = dot(feed_ref[...], w1_ref[...], 1, 0).astype(jnp.bfloat16)
-        else:
-            pre = feed_ref[...]
-        act, slope = gelu_parts(pre.astype(jnp.float32))
-        if replay:
-            outs[2][...] = act.astype(jnp.bfloat16)
-        d_act = dot(d_ref[...], w2_ref[...], 1, 1).astype(jnp.bfloat16)
-        d_pre = (d_act.astype(jnp.float32) * slope).astype(jnp.bfloat16)
-        outs[0][...] = d_pre
-        part = dot(d_pre, w1_ref[...], 1, 1)
-
-        @pl.when(i == 0)
-        def _():
-            acc_ref[...] = part
-
-        @pl.when(i > 0)
-        def _():
-            acc_ref[...] += part
-
-        @pl.when(i == steps - 1)
-        def _():
-            d_normed = acc_ref[...].astype(jnp.bfloat16).astype(jnp.float32)
-            back = rms_backward(h_ref[...].astype(jnp.float32), d_normed)
-            outs[1][...] = (d_ref[...].astype(jnp.float32) + back).astype(jnp.bfloat16)
-
-    full = whole((tokens, width))
-    up = pl.BlockSpec((width, FF_BLOCK), lambda i: (0, i))
-    down = pl.BlockSpec((FF_BLOCK, width), lambda i: (i, 0))
-    wide = pl.BlockSpec((tokens, FF_BLOCK), lambda i: (0, i))
-    outs = [(bf16(tokens, ff), wide), (bf16(tokens, width), full)] + ([(bf16(tokens, ff), wide)] if replay else [])
-    return call(
-        kernel, (steps,), [full, full, full if replay else wide, up, down], outs,
-        [pltpu.VMEM((tokens, width), jnp.float32)], flops=(6 if replay else 4) * tokens * width * ff,
-        moved=4 * tokens * ff + 4 * width * ff, name=name)(d_next, hidden, feed, w_up, w_down)
 
 
 def pair_backward(q_pair, k_pair, v_pair, d_pair, low, probs_of):
@@ -209,64 +51,209 @@
         d_side = jnp.where(mask, d_pair, 0)
         probs_16 = probs_of(side)
         probs_32 = probs_16.astype(jnp.float32)
-        d_probs = dot(d_side, v_pair, 1, 1).astype(jnp.bfloat16).astype(jnp.float32)
-        row_dot = jnp.sum(d_probs * probs_32, axis=-1, keepdims=True)
+        d_probs = dot(v_pair, d_side, 1, 1).astype(jnp.bfloat16).astype(jnp.float32)
+        row_dot = jnp.sum(d_probs * probs_32, axis=0, keepdims=True)
         d_scores = (probs_32 * (d_probs - row_dot) * HEAD_DIM ** -0.5).astype(jnp.bfloat16)
-        parts = (dot(d_scores, jnp.where(mask, k_pair, 0), 1, 0),
-                 dot(d_scores, jnp.where(mask, q_pair, 0), 0, 0),
-                 dot(probs_16, d_side, 0, 0))
+        parts = (dot(d_scores, jnp.where(mask, k_pair, 0), 0, 0),
+                 dot(d_scores, jnp.where(mask, q_pair, 0), 1, 0),
+                 dot(probs_16, d_side, 1, 0))
         sums = [part if total is None else total + part for total, part in zip(sums, parts)]
     return sums
 
 
-def attend_backward(d_hidden, query, key_act, value, probs, w_proj, layer, seq):
-    tokens, width = d_hidden.shape
+def pair_forward(q_pair, k_pair, v_pair, low, keep):
+    total = None
+    for side in range(2):
+        mask = low if side == 0 else jnp.logical_not(low)
+        scores = dot(k_pair, jnp.where(mask, q_pair, 0), 1, 1)
+        top = jnp.max(scores, axis=0, keepdims=True)
+        raised = jnp.exp2((scores - top) * SOFTMAX_SCALE)
+        inverse = 1.0 / jnp.sum(raised, axis=0, keepdims=True)
+        probs = (raised * inverse).astype(jnp.bfloat16)
+        keep(side, probs)
+        part = dot(probs, jnp.where(mask, v_pair, 0), 0, 0)
+        total = part if total is None else total + part
+    return total
+
+
+FRONT_OUTS = ("u_0", "q_0", "k_0", "v_0", "probs_0", "mixed_0", "h_0", "n_0", "pre_0", "act_0", "x_1",
+              "u_1", "mixed_1", "n_1", "act_1", "dpre_1", "dh_1", "dq_1", "dk_1", "dv_1")
+ROW_BUFFERS = ("u", "q", "k", "v", "mixed", "h", "n", "x", "dh", "dmix", "dq", "dk", "dv")
+PAIRS_AT_ONCE = 2
+WIDE_BLOCK = 1024
+
+
+def front_kernel(batch, seq, in_names, *refs):
+    at = dict(zip((*in_names, *FRONT_OUTS), refs))
+    refs = refs[len(at):]
+    x_all, cot_all, w_in, w_out, w_up, w_down, probs, pre, act = refs[:9]
+    row = dict(zip(ROW_BUFFERS, refs[9:]))
+    load_sem, out_sem = refs[9 + len(ROW_BUFFERS):]
+    width, ff = w_up.shape
     heads = width // HEAD_DIM
-
-    def kernel(d_ref, q_ref, k_ref, v_ref, p_ref, wo_ref, dq_ref, dk_ref, dv_ref, mix_ref):
-        mix_ref[...] = dot(d_ref[...], wo_ref[...], 1, 1).astype(jnp.bfloat16)
+    loads = {"x": pltpu.make_async_copy(at["x_0"], x_all, load_sem.at[0])}
+    for layer in (0, 1):
+        for i, name in enumerate(("wq", "wk", "wv")):
+            loads[f"{name}_{layer}"] = pltpu.make_async_copy(at[name].at[layer], w_in.at[layer, i], load_sem.at[1 + 4 * layer + i])
+        loads[f"wo_{layer}"] = pltpu.make_async_copy(at["wo"].at[layer], w_out.at[layer], load_sem.at[4 + 4 * layer])
+    loads["w_up"] = pltpu.make_async_copy(at["w_up"], w_up, load_sem.at[9])
+    loads["w_down"] = pltpu.make_async_copy(at["w_down"], w_down, load_sem.at[10])
+    loads["cot"] = pltpu.make_async_copy(at["cot"], cot_all, load_sem.at[11])
+    for name in ("x", "wq_0", "wk_0", "wv_0", "wo_0", "w_up", "w_down", "wq_1", "wk_1", "wv_1", "wo_1", "cot"):
+        loads[name].start()
+    holders = {"probs_0": probs, "pre_0": pre, "act_0": act, "act_1": act, "dpre_1": pre, "x_1": row["x"]}
+    for name in FRONT_OUTS:
+        holders.setdefault(name, row.get(name[:-2]))
+
+    def store(name, index):
+        src = holders[name]
+        rows = pl.ds(pl.multiple_of(seq * index, seq), seq)
+        dest = at[name].at[index] if name == "probs_0" else at[name].at[rows]
+        return pltpu.make_async_copy(src, dest, out_sem.at[FRONT_OUTS.index(name)])
+
+    def one_sequence(index, carry):
+        rows = pl.ds(pl.multiple_of(seq * index, seq), seq)
+        first = index == 0
         low = lax.broadcasted_iota(jnp.int32, (seq, PAIR), 1) < HEAD_DIM
 
-        def pair(j, carry):
-            lanes = pl.ds(pl.multiple_of(PAIR * j, PAIR), PAIR)
-            q_pair, k_pair, v_pair, d_pair = q_ref[:, lanes], k_ref[:, lanes], v_ref[:, lanes], mix_ref[:, lanes]
-            sums = pair_backward(q_pair, k_pair, v_pair, d_pair, low, lambda side: p_ref[2 * j + side])
-            for ref, total in zip((dq_ref, dk_ref, dv_ref), sums):
-                ref[:, lanes] = total.astype(jnp.bfloat16)
-            return carry
-
-        lax.fori_loop(0, heads // 2, pair, 0)
-
-    row = pl.BlockSpec((seq, width), lambda i: (i, 0))
-    weight = pl.BlockSpec((None, width, width), lambda i: (layer, 0, 0), pipeline_mode=pl.Buffered(1))
-    block = pl.BlockSpec((None, heads, seq, seq), lambda i: (i, 0, 0, 0))
-    act = (bf16(tokens, width), row)
-    return call(
-        kernel, (tokens // seq,), [row, row, row, row, block, weight], [act, act, act],
-        [pltpu.VMEM((seq, width), jnp.bfloat16)], flops=2 * tokens * width * (width + 4 * seq), moved=24 * tokens * width,
-        name=f"attend_backward_{layer}")(d_hidden, query, key_act, value, probs, w_proj)
-
-
-def project_backward(x_act, d_hidden, d_query, d_key, d_value, w_query, w_key, w_value, layer):
-    tokens, width = x_act.shape
-    steps = width // OUT_BLOCK
-
-    def kernel(x_ref, d_ref, dq_ref, dk_ref, dv_ref, wq_ref, wk_ref, wv_ref, o_ref, sum_ref):
-        i = pl.program_id(0)
-        total = dot(dq_ref[...], wq_ref[...], 1, 1) + dot(dk_ref[...], wk_ref[...], 1, 1) + dot(dv_ref[...], wv_ref[...], 1, 1)
-        sum_ref[:, pl.ds(pl.multiple_of(OUT_BLOCK * i, OUT_BLOCK), OUT_BLOCK)] = total.astype(jnp.bfloat16)
-
-        @pl.when(i == steps - 1)
-        def _():
-            back = rms_backward(x_ref[...].astype(jnp.float32), sum_ref[...].astype(jnp.float32))
-            o_ref[...] = (d_ref[...].astype(jnp.float32) + back).astype(jnp.bfloat16)
-
-    full = whole((tokens, width))
-    weight = pl.BlockSpec((None, OUT_BLOCK, width), lambda i: (layer, i, 0))
-    return call(
-        kernel, (steps,), [full] * 5 + [weight] * 3, [(bf16(tokens, width), full)],
-        [pltpu.VMEM((tokens, width), jnp.bfloat16)], flops=6 * tokens * width * width, moved=18 * tokens * width,
-        name=f"project_backward_{layer}")(x_act, d_hidden, d_query, d_key, d_value, w_query, w_key, w_value)[0]
+        def need(*names):
+            @pl.when(first)
+            def _():
+                for name in names:
+                    loads[name].wait()
+
+        def free(*names, same=False):
+            for name in names:
+                if same:
+                    store(name, index).wait()
+                else:
+                    pl.when(index > 0)(lambda name=name: store(name, index - 1).wait())
+
+        def send(*names):
+            for name in names:
+                store(name, index).start()
+
+        def over(count, fn):
+            lax.fori_loop(0, count, lambda j, carry: fn(j) or carry, 0)
+
+        def attention(layer):
+            x_in = x_all[rows] if layer == 0 else row["x"][...]
+            row["u"][...] = rms_norm(x_in.astype(jnp.float32)).astype(jnp.bfloat16)
+            for i, kind in enumerate("qkv"):
+                need(f"w{kind}_{layer}")
+                row[kind][...] = dot(row["u"][...], w_in[layer, i], 1, 0).astype(jnp.bfloat16)
+
+            def pairs(j):
+                for extra in range(PAIRS_AT_ONCE):
+                    which = PAIRS_AT_ONCE * j + extra
+                    lanes = pl.ds(pl.multiple_of(PAIR * which, PAIR), PAIR)
+
+                    def keep(side, value):
+                        probs[2 * which + side] = value
+                    out = pair_forward(row["q"][:, lanes], row["k"][:, lanes], row["v"][:, lanes], low, keep)
+                    row["mixed"][:, lanes] = out.astype(jnp.bfloat16)
+            over(heads // 2 // PAIRS_AT_ONCE, pairs)
+            need(f"wo_{layer}")
+            attn = dot(row["mixed"][...], w_out[layer], 1, 0).astype(jnp.bfloat16)
+            hidden = (x_in.astype(jnp.float32) + attn.astype(jnp.float32)).astype(jnp.bfloat16)
+            row["h"][...] = hidden
+            row["n"][...] = rms_norm(hidden.astype(jnp.float32)).astype(jnp.bfloat16)
+
+        need("x")
+        free("u_1")
+        free("dq_1", "dk_1", "dv_1", "mixed_1", "n_1", "dh_1")
+        attention(0)
+        send("u_0", "q_0", "k_0", "v_0", "probs_0", "mixed_0", "h_0", "n_0")
+        need("w_up")
+        free("act_1", "dpre_1")
+
+        def up(j):
+            lanes = pl.ds(pl.multiple_of(WIDE_BLOCK * j, WIDE_BLOCK), WIDE_BLOCK)
+            raw = dot(row["n"][...], w_up[:, lanes], 1, 0).astype(jnp.bfloat16)
+            pre[:, lanes] = raw
+            act[:, lanes] = gelu_parts(raw.astype(jnp.float32))[0].astype(jnp.bfloat16)
+        over(ff // WIDE_BLOCK, up)
+        send("pre_0", "act_0")
+        need("w_down")
+
+        def down(j):
+            lanes = pl.ds(pl.multiple_of(OUT_BLOCK * j, OUT_BLOCK), OUT_BLOCK)
+            out = dot(act[...], w_down[:, lanes], 1, 0).astype(jnp.bfloat16).astype(jnp.float32)
+            row["x"][:, lanes] = (row["h"][:, lanes].astype(jnp.float32) + out).astype(jnp.bfloat16)
+        over(width // OUT_BLOCK, down)
+        send("x_1")
+        free("u_0", "q_0", "k_0", "v_0", "probs_0", "mixed_0", "h_0", "n_0", same=True)
+        attention(1)
+        send("u_1", "mixed_1", "n_1")
+        need("cot")
+        free("pre_0", "act_0", same=True)
+
+        def both(j):
+            lanes = pl.ds(pl.multiple_of(WIDE_BLOCK * j, WIDE_BLOCK), WIDE_BLOCK)
+            raw = dot(row["n"][...], w_up[:, lanes], 1, 0).astype(jnp.bfloat16).astype(jnp.float32)
+            d_act = dot(cot_all[rows], w_down[lanes], 1, 1).astype(jnp.bfloat16).astype(jnp.float32)
+            out, slope = gelu_parts(raw)
+            act[:, lanes] = out.astype(jnp.bfloat16)
+            pre[:, lanes] = (d_act * slope).astype(jnp.bfloat16)
+        over(ff // WIDE_BLOCK, both)
+        send("act_1", "dpre_1")
+
+        def back(j):
+            lanes = pl.ds(pl.multiple_of(OUT_BLOCK * j, OUT_BLOCK), OUT_BLOCK)
+            row["dmix"][:, lanes] = dot(pre[...], w_up[lanes], 1, 1).astype(jnp.bfloat16)
+        over(width // OUT_BLOCK, back)
+        d_hidden = cot_all[rows].astype(jnp.float32) + rms_backward(
+            row["h"][...].astype(jnp.float32), row["dmix"][...].astype(jnp.float32))
+        row["dh"][...] = d_hidden.astype(jnp.bfloat16)
+        send("dh_1")
+        row["dmix"][...] = dot(row["dh"][...], w_out[1], 1, 1).astype(jnp.bfloat16)
+
+        def pairs_back(j):
+            for extra in range(PAIRS_AT_ONCE):
+                which = PAIRS_AT_ONCE * j + extra
+                lanes = pl.ds(pl.multiple_of(PAIR * which, PAIR), PAIR)
+                sums = pair_backward(*(row[name][:, lanes] for name in ("q", "k", "v", "dmix")), low,
+                                     lambda side: probs[2 * which + side])
+                for name, total in zip(("dq", "dk", "dv"), sums):
+                    row[name][:, lanes] = total.astype(jnp.bfloat16)
+        over(heads // 2 // PAIRS_AT_ONCE, pairs_back)
+        send("dq_1", "dk_1", "dv_1")
+        free("x_1", same=True)
+        return carry
+
+    lax.fori_loop(0, batch, one_sequence, 0)
+    for name in ("u_1", "mixed_1", "n_1", "act_1", "dpre_1", "dh_1", "dq_1", "dk_1", "dv_1"):
+        store(name, batch - 1).wait()
+
+
+def front(inputs, batch, seq):
+    tokens, width = inputs["x_0"].shape
+    ff = inputs["w_up"].shape[1]
+    heads = width // HEAD_DIM
+    shapes = []
+    for name in FRONT_OUTS:
+        if name == "probs_0":
+            shapes.append(bf16(batch, heads, seq, seq))
+        else:
+            shapes.append(bf16(tokens, ff if name[:-2] in ("pre", "act", "dpre") else width))
+    block = lambda *shape: pltpu.VMEM(shape, jnp.bfloat16)
+    scratch = [
+        block(tokens, width), block(tokens, width), block(2, 3, width, width), block(2, width, width), block(width, ff),
+        block(ff, width), block(heads, seq, seq), block(seq, ff), block(seq, ff),
+        *[block(seq, width) for _ in ROW_BUFFERS],
+        pltpu.SemaphoreType.DMA((12,)), pltpu.SemaphoreType.DMA((len(FRONT_OUTS),)),
+    ]
+    outs = pl.pallas_call(
+        functools.partial(front_kernel, batch, seq, tuple(inputs)),
+        out_shape=shapes,
+        in_specs=[pl.BlockSpec(memory_space=pl.ANY)] * len(inputs),
+        out_specs=[pl.BlockSpec(memory_space=pl.ANY)] * len(shapes),
+        scratch_shapes=scratch,
+        compiler_params=pltpu.CompilerParams(vmem_limit_bytes=67_043_328),
+        cost_estimate=pl.CostEstimate(flops=22 * tokens * width * ff // 2, bytes_accessed=100 * MIB, transcendentals=0),
+        name="front",
+    )(*inputs.values())
+    return dict(zip(FRONT_OUTS, outs))
 
 
 MESH = pl.DeviceIdType.MESH
@@ -317,7 +304,7 @@
 
 
 class Backward:
-    PB_1, MB, AB, PB_0 = 0, 4, 12, 21
+    PB_1, MB, AB, PB_0 = 2, 6, 14, 23
     ROWS = 256
 
     def __init__(self, at, big, total_buf, w_buf, p_buf, sem, drain):
@@ -878,6 +865,57 @@
     return dict(zip(outs, results))
 
 
+DELIVER_ROWS = 512
+DELIVER_SLOTS = 16
+DELIVER_AHEAD = 8
+
+
+def deliver(arrays):
+    def blocks_of(array):
+        lead = [(i,) for i in range(array.shape[0])] if len(array.shape) == 3 else [()]
+        rows, cols = array.shape[-2:]
+        return [(*index, pl.ds(row, DELIVER_ROWS), pl.ds(col, LANES))
+                for index in lead for row in range(0, rows, DELIVER_ROWS) for col in range(0, cols, LANES)]
+
+    work = [(i, index) for i, array in enumerate(arrays) for index in blocks_of(array)]
+    count = len(arrays)
+
+    def kernel(*refs):
+        ins, outs, buf, in_sem, out_sem = refs[:count], refs[count:2 * count], *refs[2 * count:]
+
+        def fetch(t):
+            i, index = work[t]
+            return pltpu.make_async_copy(ins[i].at[index], buf.at[t % DELIVER_SLOTS], in_sem.at[t % DELIVER_SLOTS])
+
+        def put(t):
+            i, index = work[t]
+            return pltpu.make_async_copy(buf.at[t % DELIVER_SLOTS], outs[i].at[index], out_sem.at[t % DELIVER_SLOTS])
+
+        for t in range(min(DELIVER_AHEAD, len(work))):
+            fetch(t).start()
+        for t in range(len(work)):
+            if t + DELIVER_AHEAD < len(work):
+                if t + DELIVER_AHEAD >= DELIVER_SLOTS:
+                    put(t + DELIVER_AHEAD - DELIVER_SLOTS).wait()
+                fetch(t + DELIVER_AHEAD).start()
+            fetch(t).wait()
+            put(t).start()
+        for t in range(max(0, len(work) - DELIVER_SLOTS), len(work)):
+            put(t).wait()
+
+    return pl.pallas_call(
+        kernel,
+        out_shape=[jax.ShapeDtypeStruct(array.shape, array.dtype) for array in arrays],
+        in_specs=[pl.BlockSpec(memory_space=pl.ANY)] * count,
+        out_specs=[pl.BlockSpec(memory_space=pl.ANY)] * count,
+        scratch_shapes=[pltpu.VMEM((DELIVER_SLOTS, DELIVER_ROWS, LANES), jnp.float32),
+                        pltpu.SemaphoreType.DMA((DELIVER_SLOTS,)), pltpu.SemaphoreType.DMA((DELIVER_SLOTS,))],
+        compiler_params=pltpu.CompilerParams(vmem_limit_bytes=67_043_328),
+        cost_estimate=pl.CostEstimate(flops=0, bytes_accessed=2 * sum(a.size for a in arrays) * 4, transcendentals=0),
+        name="deliver",
+    )(*arrays)
+
+
 def gradient_groups(width, ff):
     groups = []
 
@@ -907,16 +945,8 @@
     batch, seq, width = x_init.shape
     tokens = batch * seq
     at = {"x_0": x_init.reshape(tokens, width), "cot": cot_out.reshape(tokens, width)}
-    for layer in (0, 1):
-        x_in = at[f"x_{layer}"]
-        at[f"u_{layer}"], query, key_act, value = project_qkv(x_in, w_query, w_key, w_value, layer)
-        probs, at[f"mixed_{layer}"], hidden, at[f"n_{layer}"] = attend(x_in, query, key_act, value, w_proj, layer, seq)
-        if layer == 0:
-            at.update(q_0=query, k_0=key_act, v_0=value, probs_0=probs, h_0=hidden)
-            at["pre_0"], at["act_0"], at["x_1"] = mlp_forward(hidden, at["n_0"], w_up, w_down)
-    at["dpre_1"], at["dh_1"], at["act_1"] = mlp_backward(at["cot"], hidden, at["n_1"], w_up, w_down, True, "mlp_both")
-    at["dq_1"], at["dk_1"], at["dv_1"] = attend_backward(at["dh_1"], query, key_act, value, probs, w_proj, 1, seq)
     at.update(wq=w_query, wk=w_key, wv=w_value, wo=w_proj, w_up=w_up, w_down=w_down)
+    at.update(front(at, batch, seq))
     return at
 
 
@@ -927,7 +957,7 @@
         groups, chunks = gradient_groups(width, w_up.shape[1])
         weights = dict(g_q=w_query.shape, g_k=w_key.shape, g_v=w_value.shape, g_o=w_proj.shape, g_up=w_up.shape, g_down=w_down.shape)
         res = finish_backward(inputs, groups, chunks, weights, batch * seq, seq)
-        return (*(res[name] for name in weights), res["dx_0"].reshape(x_init.shape))
+        return (*deliver([res[name] for name in weights]), res["dx_0"].reshape(x_init.shape))
 
     data_spec = P("data")
     full_spec = P()

time: 672 us -> 648 us (0.964)
  local copies, waits for them, and re-layouts: 47.2 us -> 3.08 us
  Pallas kernels: 624 us -> 644 us
    unnamed x27 -> x1, local copies, waits for them, and re-layouts: 47.2 us -> 3.08 us
    pallas_call x7 -> x2, Pallas kernels: 172 us -> 193 us  [the longest x1 149 us: front(): pl.pallas_call(functools.partial(front_kernel, batch, seq, tuple(inputs))...]
where the time goes in v4:
time: 648 us; the launch traced here: 647 us
  Pallas kernels  644 us (99%)
    pallas_call x1, Pallas kernels, finish_backward(): pl.pallas_call(functools.partial(finish_kernel, groups, chunks, list(inpu...  450 us
    pallas_call x1, Pallas kernels, front(): pl.pallas_call(functools.partial(front_kernel, batch, seq, tuple(inputs))...  149 us
    pallas_call x1, Pallas kernels, deliver(): pl.pallas_call(kernel, out_shape=[jax.ShapeDtypeStruct(array.shape, array...  44.2 us

profile of v4, /device:TPU:0, one launch (start us, length us, event | category | flops | bytes accessed | tf_op | source)
XLA Modules:
  0.0 647.4 jit_solution(15231746125574545855)
XLA Ops:
  0.6 149.1 %front.1 = (bf16[1024,1024]{1,0:T(8,128)(2,1)}, bf16[1024,1024]{1,0:T(8,128)(2,1)}, bf16[1024,1024]{1,0:T(8,128)(2,1)}, bf16[1024,1024]{1,0:T(8,128)(2,1)}, bf16...) custom-call(bf16[1024,1024]{1,0:T(8,128)(2,1)} %bitcast.4, ...), custom_call_target="tpu_custom_call" | custom-call | flops 47244640256 | bytes 104857600 | tf_op jit(solution)/shard_map/front/pallas_call | solution.py:246
  149.7 450.4 %finish_backward.1 = (f32[2,1024,1024]{2,1,0:T(8,128)}, f32[2,1024,1024]{2,1,0:T(8,128)}, f32[2,1024,1024]{2,1,0:T(8,128)}, f32[2,1024,1024]{2,1,0:T(8,128)}, f3...) custom-call(bf16[1024,1024]{1,0:T(8,128)(2,1)} %bitcast.5, ...), custom_call_target="tpu_custom_call" | custom-call | flops 85899345920 | bytes 268435456 | tf_op jit(solution)/shard_map/finish_backward/pallas_call | solution.py:855
  600.1 44.2 %deliver.1 = (f32[2,1024,1024]{2,1,0:T(8,128)}, f32[2,1024,1024]{2,1,0:T(8,128)}, f32[2,1024,1024]{2,1,0:T(8,128)}, f32[2,1024,1024]{2,1,0:T(8,128)}, f32[1024,4096]{1,0:T(8,128)}, /*index=5*/f32[4096,1024]{1,0:T(8,128)}) custom-call(f32[2,1024,1024]{2,1,0:T(8,128)} %get-tuple-element.60.refs_0_, f32[2,1024,1024]{2,1,0:T(8,128)} %get-tuple-element.61.refs_1_, ...), custom_call_target="tpu_custom_call" | custom-call | bytes 134217728 | tf_op jit(solution)/shard_map/deliver/pallas_call | solution.py:906
  644.3 3.1 copy.16
